TPU v7x, 32 devices: a whole 2x2x4 slice. The times are simulated.
32 devices in a mesh: gx: 2 (over x), gy: 4 (over z), gz: 4 (over y, core).
Axes of the slice: x: 2, y: 2, z: 4, core: 2. Of those that a mesh axis runs over, the one named last changes fastest.
Arguments:
- point_frac: float32 [3, 131072], P(None, ('gx', 'gy', 'gz')), may hold values from 0.5 to 1.5
- cell_offset: int32 [3, 131072], P(None, ('gx', 'gy', 'gz')), may hold values from 0 to 3
- point_velocity: float32 [3, 131072], P(None, ('gx', 'gy', 'gz')), may hold values from -6 to 6
- point_affine: float32 [9, 131072], P(None, ('gx', 'gy', 'gz')), may hold values from -3 to 3
- point_stress: float32 [6, 131072], P(None, ('gx', 'gy', 'gz')), may hold values from -9.5 to 3, as said below
- point_mass: float32 [131072], P(('gx', 'gy', 'gz')), may hold values from 0.5 to 2
- block_tile: int32 [1024], P(('gx', 'gy', 'gz')), may hold values from 0 to 511, as said below
- block_count: int32 [1024], P(('gx', 'gy', 'gz')), may hold values from 1 to 128, as said below
Outputs:
- new_velocity: float32 [3, 131072], P(None, ('gx', 'gy', 'gz'))
- new_affine: float32 [9, 131072], P(None, ('gx', 'gy', 'gz'))
- new_stress: float32 [6, 131072], P(None, ('gx', 'gy', 'gz'))
- grid_velocity: float32 [3, 32, 256, 128], P(None, 'gx', 'gy', 'gz')
Inputs may be any that keep to these rules, and one draw needn't show every extreme that they name: `block_tile`: block b lies on the device numbered b // 32 (gz fastest, then gy, then gx) and names a tile of that device's region, t = (tx 64 / 4 + ty) * 8 + tz; a tile may be named by no block or by several. The first block_count slots of a block hold live points. `point_stress`: components in the order xx, yy, zz, yz, xz, xy.
All inputs are finite; a program needn't handle non-finite values.
Results may differ from a plain program's by a relative error of at most 0.0003.
Values sent between devices are 32-bit elements; how exact they have to be, the bound alone decides.
No kernel may reach another device: no remote copies, remote signals or barrier semaphores. Data moves between devices by JAX's collectives and lax.ppermute only.
A program may use at most 128 MiB of HBM per device.

v0:
```python
import jax
import jax.numpy as jnp
from jax import lax
from jax.experimental import pallas as pl
from jax.experimental.pallas import tpu as pltpu
from jax.sharding import PartitionSpec as P

CX = 16
CY = 64
CZ = 32
BLOCK = 128

time_step = 0.1
gravity = 1.0
shear_modulus = 2.0
bulk_modulus = 4.0
friction_static = 0.38
friction_limit = 0.64
inertial_ref = 0.28
grain_size = 0.5
grain_density = 1.0
pressure_floor = 0.5
shear_floor = 0.5
mass_floor = 0.05
stress_scale = 0.4
pair_index = ((0, 5, 4), (5, 1, 3), (4, 3, 2))
component_pairs = ((0, 0), (1, 1), (2, 2), (1, 2), (0, 2), (0, 1))

PX = CX + 2
PY = CY + 2
PZ = CZ + 2
PLANE = 4 * PZ
TILES = PX * PLANE // 8
SPAN = 5
GROUPS = -(-TILES // SPAN)
ROWS = GROUPS * SPAN * 8
REST = 2 * PY - 128
STRIDE = 40
VMEM_LIMIT = 16 * 1024 * 1024
FAR = 3.0e38


def stress_update(stress, affine):
    strain_rate = [
        [
            0.5 * (affine[3 * row_dim + col_dim] + affine[3 * col_dim + row_dim])
            for col_dim in range(3)
        ]
        for row_dim in range(3)
    ]
    volume_rate = strain_rate[0][0] + strain_rate[1][1] + strain_rate[2][2]
    deviator = [
        [
            strain_rate[row_dim][col_dim] - (volume_rate / 3.0 if row_dim == col_dim else 0.0)
            for col_dim in range(3)
        ]
        for row_dim in range(3)
    ]
    trial_stress = []
    for component in range(6):
        row_dim, col_dim = component_pairs[component]
        value = stress[component] + time_step * 2.0 * shear_modulus * deviator[row_dim][col_dim]
        if component < 3:
            value = value + time_step * bulk_modulus * volume_rate
        trial_stress.append(value)
    pressure = -(trial_stress[0] + trial_stress[1] + trial_stress[2]) / 3.0
    shear_part = [trial_stress[component] + pressure for component in range(3)] + trial_stress[3:]
    shear_stress = jnp.sqrt(
        0.5 * (shear_part[0] ** 2 + shear_part[1] ** 2 + shear_part[2] ** 2)
        + shear_part[3] ** 2
        + shear_part[4] ** 2
        + shear_part[5] ** 2
    )
    shear_rate = jnp.sqrt(
        2.0
        * (
            deviator[0][0] ** 2
            + deviator[1][1] ** 2
            + deviator[2][2] ** 2
            + 2.0 * (deviator[1][2] ** 2 + deviator[0][2] ** 2 + deviator[0][1] ** 2)
        )
    )
    inertial = (
        shear_rate * grain_size / jnp.sqrt(jnp.maximum(pressure, pressure_floor) / grain_density)
    )
    friction = friction_static + (friction_limit - friction_static) * inertial / (
        inertial_ref + inertial
    )
    support = jnp.maximum(pressure, 0.0)
    factor = jnp.minimum(1.0, friction * support / jnp.maximum(shear_stress, shear_floor))
    return [shear_part[component] * factor - support for component in range(3)] + [
        shear_part[component] * factor for component in range(3, 6)
    ]


def spline(fraction):
    left = 0.5 * (1.5 - fraction) ** 2
    middle = 0.75 - (fraction - 1.0) ** 2
    right = 0.5 * (fraction - 0.5) ** 2
    plain = (left, middle, right)
    moment = (left * (0.0 - fraction), middle * (1.0 - fraction), right * (2.0 - fraction))
    return plain, moment


def pick(masks, values):
    zero = jnp.zeros_like(values[0])
    return jnp.where(
        masks[0], values[0], jnp.where(masks[1], values[1], jnp.where(masks[2], values[2], zero))
    )


def slot_masks(slot, offset):
    shifted = slot - offset
    return (shifted == 0, shifted == 1, shifted == 2)


def x_weights(fraction, offset):
    plain, moment = spline(fraction)
    at = [offset == step for step in range(4)]
    zero = jnp.zeros_like(fraction)
    result = []
    for values in (plain, moment):
        row = []
        for slot in range(6):
            value = zero
            for node in range(3):
                if 0 <= slot - node <= 3:
                    value = jnp.where(at[slot - node], values[node], value)
            row.append(value)
        result.append(row)
    return result


def pair_weights(fraction, offset):
    plain, moment = spline(fraction)
    upper = (lax.broadcasted_iota(jnp.int32, (8, BLOCK), 0) >= 4).astype(jnp.int32)
    weight, first = [], []
    for pair in range(3):
        masks = slot_masks(upper + 2 * pair, offset)
        weight.append(pick(masks, plain))
        first.append(pick(masks, moment))
    return weight, first


def lane_weights(fraction, offset):
    plain, moment = spline(fraction)
    slot = lax.broadcasted_iota(jnp.int32, (8, BLOCK), 0)
    masks = slot_masks(slot, offset)
    return pick(masks, plain), pick(masks, moment)


def split(values):
    high = values.astype(jnp.bfloat16)
    return high, (values - high.astype(jnp.float32)).astype(jnp.bfloat16)


def point_rows(frac_ref, offset_ref, lanes):
    fraction = [jnp.broadcast_to(frac_ref[dim : dim + 1, lanes], (8, BLOCK)) for dim in range(3)]
    offset = [jnp.broadcast_to(offset_ref[dim : dim + 1, lanes], (8, BLOCK)) for dim in range(3)]
    return fraction, offset


def tile_corner(tile):
    tiles_y, tiles_z = CY // 4, CZ // 4
    tile_x = tile // (tiles_y * tiles_z)
    tile_y = (tile // tiles_z) % tiles_y
    tile_z = tile % tiles_z
    return tile_x * (4 * PLANE) + tile_z * 16, tile_y * 4


def window_rows(corner, step):
    return pl.ds(pl.multiple_of(corner + step * PLANE, 8), 24)


def lane_index():
    return lax.broadcasted_iota(jnp.int32, (8, BLOCK), 1)


def roll(values, shift):
    return pltpu.roll(values, shift % 128, 1) if shift % 128 else values


def pack_pairs(first, second, target):
    lane = lane_index()
    last = jnp.zeros((8, BLOCK), jnp.float32)
    for spot, (one, two) in enumerate(zip(first, second)):
        target[8 * spot : 8 * spot + 8, :] = jnp.where(lane < PY, one, roll(two, PY))
        last = jnp.where(lane // REST == spot, roll(two, REST * spot - (PY - REST)), last)
    target[8 * len(first) : 8 * len(first) + 8, :] = last


def unpack_pairs(source, count):
    lane = lane_index()
    last = source[8 * count : 8 * count + 8, :]
    first, second = [], []
    for spot in range(count):
        tile = source[8 * spot : 8 * spot + 8, :]
        first.append(jnp.where(lane < PY, tile, 0.0))
        tail = jnp.where(lane < PY, roll(last, (PY - REST) - REST * spot), 0.0)
        second.append(jnp.where(lane < PY - REST, roll(tile, -PY), tail))
    return first, second


def tile_rows(tile):
    return slice(8 * tile, 8 * tile + 8)


def deposit_kernel(
    blocks,
    tile_hbm,
    count_hbm,
    frac_hbm,
    offset_hbm,
    velocity_hbm,
    affine_hbm,
    stress_hbm,
    mass_hbm,
    stress_out,
    grid_ref,
    low_ref,
    high_ref,
    tile_ref,
    count_ref,
    frac_ref,
    offset_ref,
    velocity_ref,
    affine_ref,
    stress_ref,
    mass_ref,
    new_stress_ref,
    dense_ref,
    sems,
):
    sources = (
        velocity_hbm,
        affine_hbm,
        stress_hbm,
        mass_hbm,
        tile_hbm,
        count_hbm,
        frac_hbm,
        offset_hbm,
    )
    targets = (
        velocity_ref,
        affine_ref,
        stress_ref,
        mass_ref,
        tile_ref,
        count_ref,
        frac_ref,
        offset_ref,
    )
    copies = [
        pltpu.make_async_copy(source, target, sems.at[slot])
        for slot, (source, target) in enumerate(zip(sources, targets))
    ]
    for copy in copies:
        copy.start()
    grid_ref[...] = jnp.zeros_like(grid_ref)
    for copy in copies:
        copy.wait()

    def dense(component):
        return dense_ref[component * STRIDE : component * STRIDE + blocks, :]

    def put(component, values):
        dense_ref[component * STRIDE : component * STRIDE + blocks, :] = values

    for block in range(blocks):
        lanes = slice(block * BLOCK, (block + 1) * BLOCK)
        dense_ref[pl.ds(block, 3, stride=STRIDE), :] = velocity_ref[:, lanes]
        dense_ref[pl.ds(3 * STRIDE + block, 9, stride=STRIDE), :] = affine_ref[:, lanes]
        dense_ref[pl.ds(12 * STRIDE + block, 6, stride=STRIDE), :] = stress_ref[:, lanes]
    velocity = [dense(component) for component in range(3)]
    affine = [dense(3 + component) for component in range(9)]
    stress = [dense(12 + component) for component in range(6)]
    new_stress = stress_update(stress, affine)
    for component in range(6):
        put(12 + component, new_stress[component])
    mass = mass_ref[...]
    columns = [[mass * velocity[row] for row in range(3)] + [mass]]
    for col in range(3):
        columns.append(
            [
                mass * (affine[3 * row + col] - stress_scale * new_stress[pair_index[row][col]])
                for row in range(3)
            ]
            + [jnp.zeros_like(mass)]
        )
    for group in range(4):
        for channel in range(4):
            put(18 + 8 * group + channel, columns[group][channel])
            put(18 + 8 * group + 4 + channel, columns[group][channel])
    for block in range(blocks):
        lanes = slice(block * BLOCK, (block + 1) * BLOCK)
        new_stress_ref[:, lanes] = dense_ref[pl.ds(12 * STRIDE + block, 6, stride=STRIDE), :]
    stress_copy = pltpu.make_async_copy(new_stress_ref, stress_out, sems.at[len(copies)])
    stress_copy.start()

    lane = lane_index()

    def one_block(block, carry):
        lanes = pl.ds(pl.multiple_of(block * BLOCK, BLOCK), BLOCK)
        corner, corner_y = tile_corner(tile_ref[block])
        fraction, offset = point_rows(frac_ref, offset_ref, lanes)
        base, col_x, col_y, col_z = [
            dense_ref[pl.ds((18 + 8 * group) * STRIDE + block, 8, stride=STRIDE), :]
            for group in range(4)
        ]
        weight_x, first_x = x_weights(fraction[0], offset[0])
        weight_z, first_z = pair_weights(fraction[2], offset[2])
        offset_y = jnp.where(lane < count_ref[block], offset[1], -100)
        weight_y, first_y = lane_weights(fraction[1], offset_y)
        right = jnp.concatenate([weight_y, first_y], axis=1)
        flat = [base * weight_z[pair] + col_z * first_z[pair] for pair in range(3)]
        along = [col_x * weight_z[pair] for pair in range(3)]
        depth = [col_y * weight_z[pair] for pair in range(3)]
        left = jnp.concatenate(
            [
                jnp.concatenate(
                    [
                        weight_x[step] * flat[pair] + first_x[step] * along[pair]
                        for step in range(6)
                        for pair in range(3)
                    ],
                    axis=0,
                ),
                jnp.concatenate(
                    [weight_x[step] * depth[pair] for step in range(6) for pair in range(3)],
                    axis=0,
                ),
            ],
            axis=1,
        )
        left_high, left_low = split(left)
        fill = jnp.zeros((BLOCK - 8, 2 * BLOCK), jnp.float32)
        right_high, right_low = split(jnp.concatenate([right, fill], axis=0))

        def dot(one, two):
            return lax.dot_general(
                one, two, (((1,), (1,)), ((), ())), preferred_element_type=jnp.float32
            )

        sums = dot(left_high, right_high) + dot(left_low, right_high) + dot(left_high, right_low)
        for step in range(6):
            rows = window_rows(corner, step)
            grid_ref[rows, :] += pltpu.roll(sums[24 * step : 24 * step + 24], corner_y, 1)
        return carry

    lax.fori_loop(0, blocks, one_block, 0, unroll=4)

    low = [jnp.zeros((8, BLOCK), jnp.float32) for _ in range(SPAN)]
    high = [jnp.zeros((8, BLOCK), jnp.float32) for _ in range(SPAN)]
    for group in range(GROUPS):
        low_mask = lane // 2 == group
        high_mask = lane // 2 == (CY // 2 + group) % 64
        for spot in range(SPAN):
            tile = group * SPAN + spot
            if tile < TILES:
                turned = roll(grid_ref[tile_rows(tile), :], 2 * group)
                low[spot] = jnp.where(low_mask, turned, low[spot])
                high[spot] = jnp.where(high_mask, turned, high[spot])
    for spot in range(SPAN):
        low_ref[tile_rows(spot), :] = low[spot]
        high_ref[tile_rows(spot), :] = high[spot]
    stress_copy.wait()


def add_y(grid_ref, above, below, tiles):
    lane = lane_index()
    bottom, top = lane // 2 == 0, lane // 2 == CY // 2
    for tile in tiles:
        group, spot = divmod(tile, SPAN)
        lower = roll(below[spot], -CY - 2 * group)
        upper = roll(above[spot], CY - 2 * group)
        grid_ref[tile_rows(tile), :] += jnp.where(bottom, lower, jnp.where(top, upper, 0.0))


FACE = PLANE // 8


def join_y_faces(above_ref, below_ref, _, grid_ref, low_ref, high_ref):
    above = [above_ref[tile_rows(spot), :] for spot in range(SPAN)]
    below = [below_ref[tile_rows(spot), :] for spot in range(SPAN)]
    tiles = [step * FACE + side for step in range(PX) for side in (0, FACE - 1)]
    add_y(grid_ref, above, below, tiles)
    half = PX // 2
    for target, side in ((low_ref, 0), (high_ref, FACE - 1)):
        faces = [grid_ref[tile_rows(step * FACE + side), :] for step in range(PX)]
        pack_pairs(faces[:half], faces[half:], target)


def join_y_rest(above_ref, below_ref, _, grid_ref):
    above = [above_ref[tile_rows(spot), :] for spot in range(SPAN)]
    below = [below_ref[tile_rows(spot), :] for spot in range(SPAN)]
    tiles = [step * FACE + side for step in range(PX) for side in range(1, FACE - 1)]
    add_y(grid_ref, above, below, tiles)


def join_z(above_ref, below_ref, _, grid_ref, low_ref, high_ref):
    half = PX // 2
    for source, side in ((below_ref, 0), (above_ref, FACE - 1)):
        first, second = unpack_pairs(source, half)
        for step, value in enumerate(first + second):
            grid_ref[tile_rows(step * FACE + side), :] += value
    for target, start in ((low_ref, 0), (high_ref, CX)):
        planes = [
            [grid_ref[tile_rows((start + part) * FACE + spot), :] for spot in range(FACE)]
            for part in range(2)
        ]
        pack_pairs(planes[0], planes[1], target)


def place_bounds(place_ref):
    place = [place_ref[axis] for axis in range(3)]
    width = [place_ref[3 + axis] for axis in range(3)]
    at_y = lax.rem(place[1] * CY + lane_index() - 1 + width[1], width[1])
    return place, width, at_y < 2


def floor_of(at_x, width_x, low_y):
    outlet = (at_x >= width_x // 4) & (at_x < width_x - width_x // 4)
    return jnp.where(low_y & jnp.logical_not(outlet), 0.0, -FAR)


def bounds_z(at_z, depth_z):
    return jnp.where(at_z < 2, 0.0, -FAR), jnp.where(at_z >= depth_z - 2, 0.0, FAR)


def velocities(parts, floor, bounds):
    inverse = 1.0 / (parts[3] + mass_floor)
    u_x = parts[0] * inverse
    u_y = jnp.maximum(parts[1] * inverse - time_step * gravity, floor)
    u_z = parts[2] * inverse
    if bounds is not None:
        u_z = jnp.minimum(jnp.maximum(u_z, bounds[0]), bounds[1])
    return u_x, u_y, u_z


def settle_plane(place_ref, source_ref, source_row, u_ref, step, out_ref, out_step):
    place, width, low_y = place_bounds(place_ref)
    sublane = lax.broadcasted_iota(jnp.int32, (8, BLOCK), 0)
    at_x = lax.rem(place[0] * CX + step - 1 + width[0], width[0])
    floor = floor_of(at_x, width[0], low_y)
    for group in range(CZ // 8):
        start = 4 + 32 * group
        parts = [
            source_ref[pl.ds(source_row + start + channel, 8, stride=4), :] for channel in range(4)
        ]
        bounds = None
        if group in (0, CZ // 8 - 1):
            bounds = bounds_z(place[2] * CZ + 8 * group + sublane, width[2])
        values = velocities(parts, floor, bounds)
        for channel in range(3):
            u_ref[pl.ds(step * PLANE + start + channel, 8, stride=4), :] = values[channel]
            if out_step is not None:
                out_ref[channel, out_step, 8 * group : 8 * group + 8, :] = roll(
                    values[channel], -1
                )[:, 0:CY]


def settle_edges(place_ref, source_ref, source_row, u_ref, first, count):
    place, width, low_y = place_bounds(place_ref)
    sublane = lax.broadcasted_iota(jnp.int32, (8, BLOCK), 0)
    at_x = lax.rem(place[0] * CX + first + sublane - 1 + width[0], width[0])
    floor = floor_of(at_x, width[0], low_y)
    for edge in (0, CZ + 1):
        at_z = lax.rem(place[2] * CZ + edge - 1 + width[2], width[2])
        bounds = bounds_z(at_z + 0 * sublane, width[2])
        parts = [
            source_ref[pl.ds(source_row + 4 * edge + channel, count, stride=PLANE), :]
            for channel in range(4)
        ]
        values = velocities(parts, floor[0:count], [bound[0:count] for bound in bounds])
        for channel in range(3):
            start = first * PLANE + 4 * edge + channel
            u_ref[pl.ds(start, count, stride=PLANE), :] = values[channel]


def settle_kernel(place_ref, grid_ref, u_ref, out_hbm, out_ref, sem):
    def plane(step, carry):
        row = pl.multiple_of(step * PLANE, 8)
        settle_plane(place_ref, grid_ref, row, u_ref, step, out_ref, step - 2)
        return carry

    lax.fori_loop(2, CX, plane, 0, unroll=2)
    copy = pltpu.make_async_copy(out_ref, out_hbm.at[:, pl.ds(1, CX - 2)], sem)
    copy.start()
    for first in range(2, CX, 8):
        count = min(8, CX - first)
        settle_edges(place_ref, grid_ref, first * PLANE, u_ref, first, count)
    copy.wait()


def collect_kernel(
    blocks,
    place_ref,
    tile_ref,
    above_ref,
    below_ref,
    frac_ref,
    offset_ref,
    grid_ref,
    _,
    __,
    u_ref,
    out_hbm,
    velocity_hbm,
    affine_hbm,
    edge_ref,
    out_ref,
    stage_ref,
    velocity_ref,
    affine_ref,
    sems,
):
    for source, start, spot in ((below_ref, 0, 0), (above_ref, CX, 2)):
        first, second = unpack_pairs(source, FACE)
        for tile, value in enumerate(first + second):
            edge_ref[tile_rows(spot * FACE + tile), :] = (
                grid_ref[tile_rows(start * FACE + tile), :] + value
            )
    for spot, step in enumerate((0, 1, CX, CX + 1)):
        out_step = {1: 0, CX: 1}.get(step)
        settle_plane(place_ref, edge_ref, spot * PLANE, u_ref, step, out_ref, out_step)
    settle_edges(place_ref, edge_ref, 0, u_ref, 0, 2)
    settle_edges(place_ref, edge_ref, 2 * PLANE, u_ref, CX, 2)
    copies = [
        pltpu.make_async_copy(
            out_ref.at[:, pl.ds(slot, 1)],
            out_hbm.at[:, pl.ds(slot * (CX - 1), 1)],
            sems.at[slot],
        )
        for slot in range(2)
    ]
    for copy in copies:
        copy.start()
    lane = lane_index()

    def one_block(block, carry):
        lanes = pl.ds(pl.multiple_of(block * BLOCK, BLOCK), BLOCK)
        corner, corner_y = tile_corner(tile_ref[block])
        fraction, offset = point_rows(frac_ref, offset_ref, lanes)
        weight_x, first_x = x_weights(fraction[0], offset[0])
        weight_z, first_z = pair_weights(fraction[2], offset[2])
        weight_y, first_y = lane_weights(fraction[1], offset[1])
        right_high, right_low = split(jnp.concatenate([weight_y, first_y], axis=1))
        right = jnp.concatenate(
            [
                right_high.astype(jnp.float32),
                right_high.astype(jnp.float32),
                right_low.astype(jnp.float32),
                jnp.zeros((BLOCK - 24, 2 * BLOCK), jnp.float32),
            ],
            axis=0,
        ).astype(jnp.bfloat16)
        nodes = jnp.concatenate(
            [
                pltpu.roll(u_ref[window_rows(corner, step), :], (128 - corner_y) & 127, 1)
                for step in range(6)
            ],
            axis=0,
        )
        high = nodes.astype(jnp.bfloat16).astype(jnp.float32)
        low = nodes - high
        at = lax.broadcasted_iota(jnp.int32, nodes.shape, 1)
        left = jnp.where(
            at < 8, high, jnp.where(at < 16, pltpu.roll(low, 8, 1), pltpu.roll(high, 16, 1))
        ).astype(jnp.bfloat16)
        sums = lax.dot_general(
            left, right, (((1,), (0,)), ((), ())), preferred_element_type=jnp.float32
        )

        def over_x(weights, column):
            result = []
            for pair in range(3):
                total = None
                for step in range(6):
                    row = 24 * step + 8 * pair
                    term = weights[step] * sums[row : row + 8, column : column + BLOCK]
                    total = term if total is None else total + term
                result.append(total)
            return result

        def over_z(weights, values):
            total = weights[0] * values[0] + weights[1] * values[1] + weights[2] * values[2]
            return total + pltpu.roll(total, 4, 0)

        plain = over_x(weight_x, 0)
        velocity = over_z(weight_z, plain)
        columns = (
            over_z(weight_z, over_x(first_x, 0)),
            over_z(weight_z, over_x(weight_x, BLOCK)),
            over_z(first_z, plain),
        )
        velocity_ref[:, lanes] = velocity[0:3]
        for col in range(3):
            stage_ref[pl.ds(block * 16 + col, 3, stride=3), :] = 4.0 * columns[col][0:3]
        affine_ref[:, lanes] = stage_ref[pl.ds(pl.multiple_of(block * 16, 8), 9), :]
        return carry

    del lane
    lax.fori_loop(0, blocks, one_block, 0, unroll=4)
    last = [
        pltpu.make_async_copy(velocity_ref, velocity_hbm, sems.at[2]),
        pltpu.make_async_copy(affine_ref, affine_hbm, sems.at[3]),
    ]
    for copy in last:
        copy.start()
    for copy in copies + last:
        copy.wait()


def exchange(low, high, axis):
    count = lax.axis_size(axis)
    up = [(i, (i + 1) % count) for i in range(count)]
    down = [(target, source) for source, target in up]
    return lax.ppermute(low, axis, down), lax.ppermute(high, axis, up)


def shards(
    point_frac,
    cell_offset,
    point_velocity,
    point_affine,
    point_stress,
    point_mass,
    block_tile,
    block_count,
):
    blocks = block_tile.shape[0]
    points = blocks * BLOCK
    f32 = jnp.float32
    vmem = pl.BlockSpec(memory_space=pltpu.VMEM)
    smem = pl.BlockSpec(memory_space=pltpu.SMEM)
    hbm = pl.BlockSpec(memory_space=pltpu.HBM)
    params = pltpu.CompilerParams(vmem_limit_bytes=VMEM_LIMIT)
    grid_shape = jax.ShapeDtypeStruct((ROWS, BLOCK), f32)
    out_shape = jax.ShapeDtypeStruct((3, CX, CZ, CY), f32)

    def message(tiles):
        return jax.ShapeDtypeStruct((8 * tiles, BLOCK), f32)

    def cost(microseconds):
        return pl.CostEstimate(
            flops=int(microseconds * 8.0e6), bytes_accessed=1000, transcendentals=0
        )

    mass = point_mass.reshape(blocks, BLOCK)
    inputs = (
        block_tile,
        block_count,
        point_frac,
        cell_offset,
        point_velocity,
        point_affine,
        point_stress,
        mass,
    )
    new_stress, grid, low, high = pl.pallas_call(
        lambda *refs: deposit_kernel(blocks, *refs),
        out_shape=(
            jax.ShapeDtypeStruct((6, points), f32),
            grid_shape,
            message(SPAN),
            message(SPAN),
        ),
        in_specs=[hbm] * 8,
        out_specs=(hbm, vmem, vmem, vmem),
        scratch_shapes=[
            pltpu.SMEM(block_tile.shape, jnp.int32),
            pltpu.SMEM(block_count.shape, jnp.int32),
        ]
        + [pltpu.VMEM(array.shape, array.dtype) for array in inputs[2:]]
        + [
            pltpu.VMEM((6, points), f32),
            pltpu.VMEM((50 * STRIDE, BLOCK), f32),
            pltpu.SemaphoreType.DMA((9,)),
        ],
        compiler_params=params,
        cost_estimate=cost(5),
        name="deposit",
    )(*[pltpu.with_memory_space_constraint(array, pltpu.HBM) for array in inputs])
    above, below = exchange(low, high, "gy")
    grid, low, high = pl.pallas_call(
        join_y_faces,
        out_shape=(grid_shape, message(PX // 2 + 1), message(PX // 2 + 1)),
        in_specs=[vmem] * 3,
        out_specs=(vmem,) * 3,
        input_output_aliases={2: 0},
        compiler_params=params,
        cost_estimate=cost(0.3),
        name="join_y_faces",
    )(above, below, grid)
    grid = pl.pallas_call(
        join_y_rest,
        out_shape=grid_shape,
        in_specs=[vmem] * 3,
        out_specs=vmem,
        input_output_aliases={2: 0},
        compiler_params=params,
        cost_estimate=cost(1),
        name="join_y_rest",
    )(above, below, grid)
    above, below = exchange(low, high, "gz")
    grid, low, high = pl.pallas_call(
        join_z,
        out_shape=(grid_shape, message(FACE + 1), message(FACE + 1)),
        in_specs=[vmem] * 3,
        out_specs=(vmem,) * 3,
        input_output_aliases={2: 0},
        compiler_params=params,
        cost_estimate=cost(0.3),
        name="join_z",
    )(above, below, grid)
    above, below = exchange(low, high, "gx")
    place = jnp.stack(
        [lax.axis_index("gx"), lax.axis_index("gy"), lax.axis_index("gz")]
        + [
            jnp.int32(lax.axis_size("gx") * CX),
            jnp.int32(lax.axis_size("gy") * CY),
            jnp.int32(lax.axis_size("gz") * CZ),
        ]
    )
    speed, grid_velocity = pl.pallas_call(
        settle_kernel,
        out_shape=(grid_shape, out_shape),
        in_specs=[smem, vmem],
        out_specs=(vmem, hbm),
        scratch_shapes=[pltpu.VMEM((3, CX - 2, CZ, CY), f32), pltpu.SemaphoreType.DMA],
        compiler_params=params,
        cost_estimate=cost(2),
        name="settle",
    )(place, grid)
    _, grid_velocity, new_velocity, new_affine = pl.pallas_call(
        lambda *refs: collect_kernel(blocks, *refs),
        out_shape=(
            grid_shape,
            out_shape,
            jax.ShapeDtypeStruct((3, points), f32),
            jax.ShapeDtypeStruct((9, points), f32),
        ),
        in_specs=[smem, smem] + [vmem] * 6 + [hbm],
        out_specs=(vmem, hbm, hbm, hbm),
        input_output_aliases={7: 0, 8: 1},
        scratch_shapes=[
            pltpu.VMEM((4 * PLANE, BLOCK), f32),
            pltpu.VMEM((3, 2, CZ, CY), f32),
            pltpu.VMEM((blocks * 16, BLOCK), f32),
            pltpu.VMEM((3, points), f32),
            pltpu.VMEM((9, points), f32),
            pltpu.SemaphoreType.DMA((4,)),
        ],
        compiler_params=params,
        cost_estimate=cost(4),
        name="collect",
    )(place, block_tile, above, below, point_frac, cell_offset, grid, speed, grid_velocity)
    return (new_velocity, new_affine, new_stress, grid_velocity.transpose(0, 1, 3, 2))


def solution(mesh):
    points = ("gx", "gy", "gz")
    return jax.shard_map(
        shards,
        mesh=mesh,
        in_specs=(P(None, points),) * 5 + (P(points),) * 3,
        out_specs=(P(None, points),) * 3 + (P(None, "gx", "gy", "gz"),),
        check_vma=False,
    )
```

profile of v0, /device:TPU:0, one launch (start us, length us, event | category | flops | bytes accessed | tf_op | source)
XLA Modules:
  0.0 32.5 jit_solution(13563785040299819384)
XLA Ops:
  0.6 5.6 %deposit.1 = (f32[6,4096]{1,0:T(8,128)}, f32[2480,128]{1,0:T(8,128)S(1)}, f32[40,128]{1,0:T(8,128)S(1)}, f32[40,128]{1,0:T(8,128)S(1)}) custom-call(s32[32]{0:T(128)} %refs_1_.3, s32[32]{0:T(128)} %refs_1_.2, f32[3,4096]{1,0:T(4,128)} %refs_4_.3, s32[3,4096]{1,0:T(4,128)} %refs_5_.3, f32[3,4096]{1,0:T(4,128)} %refs_4_.2, f32[9,4096]{1,0:T(8,128)} %refs_5_.2, ...), custom_call_target="tpu_custom_call" | custom-call | flops 40000000 | bytes 1000 | tf_op jit(solution)/shard_map/deposit/pallas_call | solution.py:661
  6.2 5.1 %collective-permute-start = (f32[40,128]{1,0:T(8,128)S(1)}, f32[40,128]{1,0:T(8,128)S(1)}, u32[]{:S(2)}, u32[]{:S(2)}) collective-permute-start(f32[40,128]{1,0:T(8,128)S(1)} %get-tuple-element.19), channel_id=1, source_target_pairs={{4,0},{8,4},{12,8},{0,12},{5,1},{9,5},{13,9},{1,13},{6,2},{10,6},{... | collective-permute-start | bytes 61448 | tf_op jit(solution)/shard_map/ppermute | solution.py:619
  11.3 0.0 collective-permute-start.1
  11.4 1.5 %collective-permute-done.above_ref = f32[40,128]{1,0:T(8,128)S(1)} collective-permute-done((f32[40,128]{1,0:T(8,128)S(1)}, f32[40,128]{1,0:T(8,128)S(1)}, u32[]{:S(2)}, u32[]{:S(2)}) %collective-permute-start) | collective-permute-done | bytes 20512 | tf_op jit(solution)/shard_map/ppermute | solution.py:619
  12.8 4.1 %collective-permute-done.1.below_ref = f32[40,128]{1,0:T(8,128)S(1)} collective-permute-done((f32[40,128]{1,0:T(8,128)S(1)}, f32[40,128]{1,0:T(8,128)S(1)}, u32[]{:S(2)}, u32[]{:S(2)}) %collective-permute-start.1) | collective-permute-done | bytes 20512 | tf_op jit(solution)/shard_map/ppermute | solution.py:619
  16.9 0.2 join_y_faces.1
  17.2 0.1 collective-permute-start.2
  17.2 0.5 %collective-permute-start.3 = (f32[80,128]{1,0:T(8,128)S(1)}, f32[80,128]{1,0:T(8,128)S(1)}, u32[]{:S(2)}, u32[]{:S(2)}) collective-permute-start(f32[80,128]{1,0:T(8,128)S(1)} %get-tuple-element.23), channel_id=1, source_target_pairs={{0,1},{1,2},{2,3},{3,0},{4,5},{5,6},{6,7},{7,4},{8,9},{9,10},{10,1... | collective-permute-start | bytes 122888 | tf_op jit(solution)/shard_map/ppermute | solution.py:619
  17.7 0.6 %join_y_rest.1._ = f32[2480,128]{1,0:T(8,128)S(1)} custom-call(f32[40,128]{1,0:T(8,128)S(1)} %collective-permute-done.above_ref, f32[40,128]{1,0:T(8,128)S(1)} %collective-permute-done.1.below_ref, f32[2480,128]{1,0:T(8,128)S(1)} %get-tuple-element.24._), custom_call_target="tpu_custom_call", output_to_operand_aliasing={{}: (2, {})} | custom-call | flops 8000000 | bytes 1000 | tf_op jit(solution)/shard_map/join_y_rest/pallas_call | solution.py:696
  18.3 0.0 copy-start
  18.4 0.0 copy-start.1
  18.4 0.0 copy-start.2
  18.4 0.5 %collective-permute-done.2.above_ref = f32[80,128]{1,0:T(8,128)S(1)} collective-permute-done((f32[80,128]{1,0:T(8,128)S(1)}, f32[80,128]{1,0:T(8,128)S(1)}, u32[]{:S(2)}, u32[]{:S(2)}) %collective-permute-start.2) | collective-permute-done | bytes 40992 | tf_op jit(solution)/shard_map/ppermute | solution.py:619
  18.9 2.2 %collective-permute-done.3.below_ref = f32[80,128]{1,0:T(8,128)S(1)} collective-permute-done((f32[80,128]{1,0:T(8,128)S(1)}, f32[80,128]{1,0:T(8,128)S(1)}, u32[]{:S(2)}, u32[]{:S(2)}) %collective-permute-start.3) | collective-permute-done | bytes 40992 | tf_op jit(solution)/shard_map/ppermute | solution.py:619
  21.1 0.2 join_z.1
  21.3 1.6 %collective-permute-start.4 = (f32[144,128]{1,0:T(8,128)S(1)}, f32[144,128]{1,0:T(8,128)S(1)}, u32[]{:S(2)}, u32[]{:S(2)}) collective-permute-start(f32[144,128]{1,0:T(8,128)S(1)} %get-tuple-element.25), channel_id=1, source_target_pairs={{16,0},{0,16},{17,1},{1,17},{18,2},{2,18},{19,3},{3,19},{20,4},{4,... | collective-permute-start | bytes 221192 | tf_op jit(solution)/shard_map/ppermute | solution.py:619
  22.9 0.5 %collective-permute-start.5 = (f32[144,128]{1,0:T(8,128)S(1)}, f32[144,128]{1,0:T(8,128)S(1)}, u32[]{:S(2)}, u32[]{:S(2)}) collective-permute-start(f32[144,128]{1,0:T(8,128)S(1)} %get-tuple-element.26), channel_id=1, source_target_pairs={{0,16},{16,0},{1,17},{17,1},{2,18},{18,2},{3,19},{19,3},{4,20},{20... | collective-permute-start | bytes 221192 | tf_op jit(solution)/shard_map/ppermute | solution.py:619
  23.4 0.1 stack.15.place_ref.refs_0_
  23.5 2.9 %settle.1 = (f32[2480,128]{1,0:T(8,128)S(1)}, f32[3,16,32,64]{3,2,1,0:T(8,128)}) custom-call(s32[6]{0:T(128)S(1)} %stack.15.place_ref.refs_0_, f32[2480,128]{1,0:T(8,128)S(1)} %get-tuple-element.27.grid_ref.refs_6_), custom_call_target="tpu_custom_call" | custom-call | flops 16000000 | bytes 1000 | tf_op jit(solution)/shard_map/settle/pallas_call | solution.py:726
  26.4 0.0 collective-permute-done.4.refs_2_
  26.4 0.9 %collective-permute-done.5.refs_3_ = f32[144,128]{1,0:T(8,128)S(1)} collective-permute-done((f32[144,128]{1,0:T(8,128)S(1)}, f32[144,128]{1,0:T(8,128)S(1)}, u32[]{:S(2)}, u32[]{:S(2)}) %collective-permute-start.5) | collective-permute-done | bytes 73760 | tf_op jit(solution)/shard_map/ppermute | solution.py:619
  27.3 0.0 copy-done
  27.3 0.0 copy-done.1
  27.3 0.0 copy-done.2
  27.3 5.2 %collect.1 = (f32[2480,128]{1,0:T(8,128)S(1)}, f32[3,16,32,64]{3,2,1,0:T(8,128)}, f32[3,4096]{1,0:T(4,128)}, f32[9,4096]{1,0:T(8,128)}) custom-call(s32[6]{0:T(128)S(1)} %stack.15.place_ref.refs_0_, s32[32]{0:T(128)S(1)} %copy-done.2, f32[144,128]{1,0:T(8,128)S(1)} %collective-permute-done.4.refs_2_, ...), custom_call_target="tpu_custom_call", output_to_operand_aliasing={{0}: (7, {}), {1}: (8, {})} | custom-call | flops 32000000 | bytes 1000 | tf_op jit(solution)/shard_map/collect/pallas_call | solution.py:736
Async XLA Ops:
  6.2 6.6 %collective-permute-start = (f32[40,128]{1,0:T(8,128)S(1)}, f32[40,128]{1,0:T(8,128)S(1)}, u32[]{:S(2)}, u32[]{:S(2)}) collective-permute-start(f32[40,128]{1,0:T(8,128)S(1)} %get-tuple-element.19), channel_id=1, source_target_pairs={{4,0},{8,4},{12,8},{0,12},{5,1},{9,5},{13,9},{1,13},{6,2},{10,6},{... | collective-permute-start | bytes 61448 | tf_op jit(solution)/shard_map/ppermute | solution.py:619
  11.3 5.6 %collective-permute-start.1 = (f32[40,128]{1,0:T(8,128)S(1)}, f32[40,128]{1,0:T(8,128)S(1)}, u32[]{:S(2)}, u32[]{:S(2)}) collective-permute-start(f32[40,128]{1,0:T(8,128)S(1)} %get-tuple-element.20), channel_id=1, source_target_pairs={{0,4},{4,8},{8,12},{12,0},{1,5},{5,9},{9,13},{13,1},{2,6},{6,10},{... | collective-permute-start | bytes 61448 | tf_op jit(solution)/shard_map/ppermute | solution.py:619
  17.2 1.7 %collective-permute-start.2 = (f32[80,128]{1,0:T(8,128)S(1)}, f32[80,128]{1,0:T(8,128)S(1)}, u32[]{:S(2)}, u32[]{:S(2)}) collective-permute-start(f32[80,128]{1,0:T(8,128)S(1)} %get-tuple-element.22), channel_id=1, source_target_pairs={{1,0},{2,1},{3,2},{0,3},{5,4},{6,5},{7,6},{4,7},{9,8},{10,9},{11,1... | collective-permute-start | bytes 122888 | tf_op jit(solution)/shard_map/ppermute | solution.py:619
  17.2 3.9 %collective-permute-start.3 = (f32[80,128]{1,0:T(8,128)S(1)}, f32[80,128]{1,0:T(8,128)S(1)}, u32[]{:S(2)}, u32[]{:S(2)}) collective-permute-start(f32[80,128]{1,0:T(8,128)S(1)} %get-tuple-element.23), channel_id=1, source_target_pairs={{0,1},{1,2},{2,3},{3,0},{4,5},{5,6},{6,7},{7,4},{8,9},{9,10},{10,1... | collective-permute-start | bytes 122888 | tf_op jit(solution)/shard_map/ppermute | solution.py:619
  18.3 9.0 %copy-start = (f32[3,4096]{1,0:T(4,128)S(1)}, f32[3,4096]{1,0:T(4,128)}, u32[]{:S(2)}) copy-start(f32[3,4096]{1,0:T(4,128)} %refs_4_.3) | copy-start | bytes 147460
  18.4 9.0 %copy-start.1 = (s32[3,4096]{1,0:T(4,128)S(1)}, s32[3,4096]{1,0:T(4,128)}, u32[]{:S(2)}) copy-start(s32[3,4096]{1,0:T(4,128)} %refs_5_.3) | copy-start | bytes 147460
  18.4 8.9 %copy-start.2 = (s32[32]{0:T(128)S(1)}, s32[32]{0:T(128)}, u32[]{:S(2)}) copy-start(s32[32]{0:T(128)} %refs_1_.3) | copy-start | bytes 388
  21.3 5.0 %collective-permute-start.4 = (f32[144,128]{1,0:T(8,128)S(1)}, f32[144,128]{1,0:T(8,128)S(1)}, u32[]{:S(2)}, u32[]{:S(2)}) collective-permute-start(f32[144,128]{1,0:T(8,128)S(1)} %get-tuple-element.25), channel_id=1, source_target_pairs={{16,0},{0,16},{17,1},{1,17},{18,2},{2,18},{19,3},{3,19},{20,4},{4,... | collective-permute-start | bytes 221192 | tf_op jit(solution)/shard_map/ppermute | solution.py:619
  22.9 4.4 %collective-permute-start.5 = (f32[144,128]{1,0:T(8,128)S(1)}, f32[144,128]{1,0:T(8,128)S(1)}, u32[]{:S(2)}, u32[]{:S(2)}) collective-permute-start(f32[144,128]{1,0:T(8,128)S(1)} %get-tuple-element.26), channel_id=1, source_target_pairs={{0,16},{16,0},{1,17},{17,1},{2,18},{18,2},{3,19},{19,3},{4,20},{20... | collective-permute-start | bytes 221192 | tf_op jit(solution)/shard_map/ppermute | solution.py:619
where the time goes:
time: 32.7 us; the launch traced here: 32.5 us
  Pallas kernels  14.7 us (45%)
  waiting for transfers between devices  9.26 us (28%)
  starting transfers between devices  7.78 us (24%)
  between operations  0.72 us (2%)
    ppermute x6, waiting for transfers between devices, exchange(): return (lax.ppermute(low, axis, down), lax.ppermute(high, axis, up))  9.26 us
    ppermute x6, starting transfers between devices, exchange(): return (lax.ppermute(low, axis, down), lax.ppermute(high, axis, up))  7.78 us
    pallas_call x1, Pallas kernels, shards(): pl.pallas_call(lambda *refs: deposit_kernel(blocks, *refs), out_shape=(ja...  5.58 us
    pallas_call x1, Pallas kernels, shards(): pl.pallas_call(lambda *refs: collect_kernel(blocks, *refs), out_shape=(gr...  5.21 us
    pallas_call x1, Pallas kernels, shards(): pl.pallas_call(settle_kernel, out_shape=(grid_shape, out_shape), in_specs...  2.86 us
  transfers between devices with their start and end apart: 6, of which 5 were waited for; matrix products, arithmetic and copies ran while one was open for 0% of the time, Pallas kernels for 11%

commit v1 on v0

--- a/solution.py
+++ b/solution.py
@@ -36,6 +36,7 @@
 ROWS = GROUPS * SPAN * 8
 REST = 2 * PY - 128
 STRIDE = 40
+CHUNK = 16
 VMEM_LIMIT = 16 * 1024 * 1024
 FAR = 3.0e38
 
@@ -166,6 +167,22 @@
     tile_y = (tile // tiles_z) % tiles_y
     tile_z = tile % tiles_z
     return tile_x * (4 * PLANE) + tile_z * 16, tile_y * 4
+
+
+def expansion():
+    row = lax.broadcasted_iota(jnp.int32, (2 * BLOCK, 2 * BLOCK), 0)
+    col = lax.broadcasted_iota(jnp.int32, (2 * BLOCK, 2 * BLOCK), 1)
+    source = (col // 16) * 4 + col % 8 + jnp.where(col % 16 < 8, 0, BLOCK)
+    return jnp.where(row == source, 1.0, 0.0).astype(jnp.bfloat16)
+
+
+def expand(values, matrix, spread_ref, row):
+    wide = jnp.dot(
+        jnp.concatenate(split(values), axis=1), matrix, preferred_element_type=jnp.float32
+    )
+    count = values.shape[0]
+    spread_ref[pl.ds(pl.multiple_of(row, 8), count), :] = wide[:, 0:BLOCK]
+    spread_ref[pl.ds(pl.multiple_of(row + PX * PLANE, 8), count), :] = wide[:, BLOCK:]
 
 
 def window_rows(corner, step):
@@ -348,7 +365,7 @@
             grid_ref[rows, :] += pltpu.roll(sums[24 * step : 24 * step + 24], corner_y, 1)
         return carry
 
-    lax.fori_loop(0, blocks, one_block, 0, unroll=4)
+    lax.fori_loop(0, blocks, one_block, 0, unroll=min(blocks, 32))
 
     low = [jnp.zeros((8, BLOCK), jnp.float32) for _ in range(SPAN)]
     high = [jnp.zeros((8, BLOCK), jnp.float32) for _ in range(SPAN)]
@@ -412,9 +429,10 @@
         pack_pairs(planes[0], planes[1], target)
 
 
-def place_bounds(place_ref):
-    place = [place_ref[axis] for axis in range(3)]
-    width = [place_ref[3 + axis] for axis in range(3)]
+def place_bounds():
+    axes = ("gx", "gy", "gz")
+    place = [lax.axis_index(axis) for axis in axes]
+    width = [lax.axis_size(axis) * cells for axis, cells in zip(axes, (CX, CY, CZ))]
     at_y = lax.rem(place[1] * CY + lane_index() - 1 + width[1], width[1])
     return place, width, at_y < 2
 
@@ -438,8 +456,9 @@
     return u_x, u_y, u_z
 
 
-def settle_plane(place_ref, source_ref, source_row, u_ref, step, out_ref, out_step):
-    place, width, low_y = place_bounds(place_ref)
+def settle_plane(source_ref, source_row, u_ref, step, out_ref, out_step, spot=None):
+    spot = step if spot is None else spot
+    place, width, low_y = place_bounds()
     sublane = lax.broadcasted_iota(jnp.int32, (8, BLOCK), 0)
     at_x = lax.rem(place[0] * CX + step - 1 + width[0], width[0])
     floor = floor_of(at_x, width[0], low_y)
@@ -453,15 +472,16 @@
             bounds = bounds_z(place[2] * CZ + 8 * group + sublane, width[2])
         values = velocities(parts, floor, bounds)
         for channel in range(3):
-            u_ref[pl.ds(step * PLANE + start + channel, 8, stride=4), :] = values[channel]
+            u_ref[pl.ds(spot * PLANE + start + channel, 8, stride=4), :] = values[channel]
             if out_step is not None:
                 out_ref[channel, out_step, 8 * group : 8 * group + 8, :] = roll(
                     values[channel], -1
                 )[:, 0:CY]
 
 
-def settle_edges(place_ref, source_ref, source_row, u_ref, first, count):
-    place, width, low_y = place_bounds(place_ref)
+def settle_edges(source_ref, source_row, u_ref, first, count, spot=None):
+    spot = first if spot is None else spot
+    place, width, low_y = place_bounds()
     sublane = lax.broadcasted_iota(jnp.int32, (8, BLOCK), 0)
     at_x = lax.rem(place[0] * CX + first + sublane - 1 + width[0], width[0])
     floor = floor_of(at_x, width[0], low_y)
@@ -474,47 +494,60 @@
         ]
         values = velocities(parts, floor[0:count], [bound[0:count] for bound in bounds])
         for channel in range(3):
-            start = first * PLANE + 4 * edge + channel
+            start = spot * PLANE + 4 * edge + channel
             u_ref[pl.ds(start, count, stride=PLANE), :] = values[channel]
 
 
-def settle_kernel(place_ref, grid_ref, u_ref, out_hbm, out_ref, sem):
+def settle_kernel(grid_ref, spread_ref, out_ref, matrix_ref, u_ref):
     def plane(step, carry):
         row = pl.multiple_of(step * PLANE, 8)
-        settle_plane(place_ref, grid_ref, row, u_ref, step, out_ref, step - 2)
+        settle_plane(grid_ref, row, u_ref, step, out_ref, step - 1)
         return carry
 
-    lax.fori_loop(2, CX, plane, 0, unroll=2)
-    copy = pltpu.make_async_copy(out_ref, out_hbm.at[:, pl.ds(1, CX - 2)], sem)
-    copy.start()
+    matrix_ref[...] = expansion()
+    lax.fori_loop(2, CX, plane, 0, unroll=7)
     for first in range(2, CX, 8):
         count = min(8, CX - first)
-        settle_edges(place_ref, grid_ref, first * PLANE, u_ref, first, count)
-    copy.wait()
+        settle_edges(grid_ref, first * PLANE, u_ref, first, count)
+
+    def spread(step, carry):
+        row = pl.multiple_of(step * PLANE, 8)
+        expand(u_ref[pl.ds(row, PLANE), :], matrix_ref[...], spread_ref, row)
+        return carry
+
+    lax.fori_loop(2, CX, spread, 0, unroll=7)
 
 
 def collect_kernel(
     blocks,
-    place_ref,
-    tile_ref,
+    tile_hbm,
     above_ref,
     below_ref,
     frac_ref,
     offset_ref,
     grid_ref,
+    inner_ref,
+    matrix_ref,
     _,
-    __,
-    u_ref,
+    spread_ref,
     out_hbm,
     velocity_hbm,
     affine_hbm,
     edge_ref,
+    u_ref,
     out_ref,
     stage_ref,
     velocity_ref,
     affine_ref,
+    tile_ref,
     sems,
 ):
+    tile_copy = pltpu.make_async_copy(tile_hbm, tile_ref, sems.at[3 + 2 * (blocks // CHUNK)])
+    tile_copy.start()
+    inner = pltpu.make_async_copy(
+        inner_ref.at[:, pl.ds(1, CX - 2)], out_hbm.at[:, pl.ds(1, CX - 2)], sems.at[2]
+    )
+    inner.start()
     for source, start, spot in ((below_ref, 0, 0), (above_ref, CX, 2)):
         first, second = unpack_pairs(source, FACE)
         for tile, value in enumerate(first + second):
@@ -523,9 +556,13 @@
             )
     for spot, step in enumerate((0, 1, CX, CX + 1)):
         out_step = {1: 0, CX: 1}.get(step)
-        settle_plane(place_ref, edge_ref, spot * PLANE, u_ref, step, out_ref, out_step)
-    settle_edges(place_ref, edge_ref, 0, u_ref, 0, 2)
-    settle_edges(place_ref, edge_ref, 2 * PLANE, u_ref, CX, 2)
+        settle_plane(edge_ref, spot * PLANE, u_ref, step, out_ref, out_step, spot)
+    settle_edges(edge_ref, 0, u_ref, 0, 2)
+    settle_edges(edge_ref, 2 * PLANE, u_ref, CX, 2, 2)
+    matrix = matrix_ref[...]
+    for spot, step in ((0, 0), (2, CX)):
+        values = u_ref[spot * PLANE : (spot + 2) * PLANE, :]
+        expand(values, matrix, spread_ref, step * PLANE)
     copies = [
         pltpu.make_async_copy(
             out_ref.at[:, pl.ds(slot, 1)],
@@ -536,9 +573,9 @@
     ]
     for copy in copies:
         copy.start()
-    lane = lane_index()
-
-    def one_block(block, carry):
+    copies.append(inner)
+
+    def one_block(block):
         lanes = pl.ds(pl.multiple_of(block * BLOCK, BLOCK), BLOCK)
         corner, corner_y = tile_corner(tile_ref[block])
         fraction, offset = point_rows(frac_ref, offset_ref, lanes)
@@ -546,31 +583,26 @@
         weight_z, first_z = pair_weights(fraction[2], offset[2])
         weight_y, first_y = lane_weights(fraction[1], offset[1])
         right_high, right_low = split(jnp.concatenate([weight_y, first_y], axis=1))
-        right = jnp.concatenate(
-            [
-                right_high.astype(jnp.float32),
-                right_high.astype(jnp.float32),
-                right_low.astype(jnp.float32),
-                jnp.zeros((BLOCK - 24, 2 * BLOCK), jnp.float32),
-            ],
+        right_high = right_high.astype(jnp.float32)
+        fill = jnp.zeros((BLOCK - 16, 2 * BLOCK), jnp.float32)
+        right_one = jnp.concatenate([right_high, right_high, fill], axis=0)
+        right_two = jnp.concatenate(
+            [right_low.astype(jnp.float32), jnp.zeros_like(right_high), fill], axis=0
+        )
+        half = corner_y // 32
+        corner = corner + half * (PX * PLANE)
+        turn = (128 - 4 * (corner_y - 32 * half)) & 127
+        left = jnp.concatenate(
+            [pltpu.roll(spread_ref[window_rows(corner, step), :], turn, 1) for step in range(6)],
             axis=0,
         ).astype(jnp.bfloat16)
-        nodes = jnp.concatenate(
-            [
-                pltpu.roll(u_ref[window_rows(corner, step), :], (128 - corner_y) & 127, 1)
-                for step in range(6)
-            ],
-            axis=0,
-        )
-        high = nodes.astype(jnp.bfloat16).astype(jnp.float32)
-        low = nodes - high
-        at = lax.broadcasted_iota(jnp.int32, nodes.shape, 1)
-        left = jnp.where(
-            at < 8, high, jnp.where(at < 16, pltpu.roll(low, 8, 1), pltpu.roll(high, 16, 1))
-        ).astype(jnp.bfloat16)
-        sums = lax.dot_general(
-            left, right, (((1,), (0,)), ((), ())), preferred_element_type=jnp.float32
-        )
+
+        def dot(right):
+            return jnp.dot(
+                left, right.astype(jnp.bfloat16), preferred_element_type=jnp.float32
+            )
+
+        sums = dot(right_one) + dot(right_two)
 
         def over_x(weights, column):
             result = []
@@ -594,21 +626,38 @@
             over_z(weight_z, over_x(weight_x, BLOCK)),
             over_z(first_z, plain),
         )
-        velocity_ref[:, lanes] = velocity[0:3]
-        for col in range(3):
-            stage_ref[pl.ds(block * 16 + col, 3, stride=3), :] = 4.0 * columns[col][0:3]
-        affine_ref[:, lanes] = stage_ref[pl.ds(pl.multiple_of(block * 16, 8), 9), :]
+        return block, lanes, velocity, columns
+
+    chunk_count = blocks // CHUNK
+    tile_copy.wait()
+
+    def chunk_copies(chunk):
+        part = pl.ds(pl.multiple_of(chunk * (CHUNK * BLOCK), BLOCK), CHUNK * BLOCK)
+        return [
+            pltpu.make_async_copy(
+                source.at[:, part], target.at[:, part], sems.at[3 + side * chunk_count + chunk]
+            )
+            for side, (source, target) in enumerate(
+                ((velocity_ref, velocity_hbm), (affine_ref, affine_hbm))
+            )
+        ]
+
+    def one_chunk(chunk, carry):
+        results = [one_block(chunk * CHUNK + spot) for spot in range(CHUNK)]
+        for block, lanes, velocity, columns in results:
+            velocity_ref[:, lanes] = velocity[0:3]
+            for col in range(3):
+                stage_ref[pl.ds(block * 16 + col, 3, stride=3), :] = 4.0 * columns[col][0:3]
+        for block, lanes, _, _ in results:
+            affine_ref[:, lanes] = stage_ref[pl.ds(pl.multiple_of(block * 16, 8), 9), :]
+        for copy in chunk_copies(chunk):
+            copy.start()
         return carry
 
-    del lane
-    lax.fori_loop(0, blocks, one_block, 0, unroll=4)
-    last = [
-        pltpu.make_async_copy(velocity_ref, velocity_hbm, sems.at[2]),
-        pltpu.make_async_copy(affine_ref, affine_hbm, sems.at[3]),
-    ]
-    for copy in last:
-        copy.start()
-    for copy in copies + last:
+    lax.fori_loop(0, chunk_count, one_chunk, 0)
+    for chunk in range(chunk_count):
+        copies += chunk_copies(chunk)
+    for copy in copies:
         copy.wait()
 
 
@@ -633,7 +682,6 @@
     points = blocks * BLOCK
     f32 = jnp.float32
     vmem = pl.BlockSpec(memory_space=pltpu.VMEM)
-    smem = pl.BlockSpec(memory_space=pltpu.SMEM)
     hbm = pl.BlockSpec(memory_space=pltpu.HBM)
     params = pltpu.CompilerParams(vmem_limit_bytes=VMEM_LIMIT)
     grid_shape = jax.ShapeDtypeStruct((ROWS, BLOCK), f32)
@@ -715,47 +763,46 @@
         name="join_z",
     )(above, below, grid)
     above, below = exchange(low, high, "gx")
-    place = jnp.stack(
-        [lax.axis_index("gx"), lax.axis_index("gy"), lax.axis_index("gz")]
-        + [
-            jnp.int32(lax.axis_size("gx") * CX),
-            jnp.int32(lax.axis_size("gy") * CY),
-            jnp.int32(lax.axis_size("gz") * CZ),
-        ]
-    )
-    speed, grid_velocity = pl.pallas_call(
+    spread_shape = message(2 * TILES)
+    spread, inner, matrix = pl.pallas_call(
         settle_kernel,
-        out_shape=(grid_shape, out_shape),
-        in_specs=[smem, vmem],
-        out_specs=(vmem, hbm),
-        scratch_shapes=[pltpu.VMEM((3, CX - 2, CZ, CY), f32), pltpu.SemaphoreType.DMA],
+        out_shape=(
+            spread_shape,
+            out_shape,
+            jax.ShapeDtypeStruct((2 * BLOCK, 2 * BLOCK), jnp.bfloat16),
+        ),
+        in_specs=[vmem],
+        out_specs=(vmem, vmem, vmem),
+        scratch_shapes=[pltpu.VMEM((PX * PLANE, BLOCK), f32)],
         compiler_params=params,
         cost_estimate=cost(2),
         name="settle",
-    )(place, grid)
+    )(grid)
     _, grid_velocity, new_velocity, new_affine = pl.pallas_call(
         lambda *refs: collect_kernel(blocks, *refs),
         out_shape=(
-            grid_shape,
+            spread_shape,
             out_shape,
             jax.ShapeDtypeStruct((3, points), f32),
             jax.ShapeDtypeStruct((9, points), f32),
         ),
-        in_specs=[smem, smem] + [vmem] * 6 + [hbm],
+        in_specs=[hbm] + [vmem] * 8,
         out_specs=(vmem, hbm, hbm, hbm),
-        input_output_aliases={7: 0, 8: 1},
+        input_output_aliases={8: 0},
         scratch_shapes=[
+            pltpu.VMEM((4 * PLANE, BLOCK), f32),
             pltpu.VMEM((4 * PLANE, BLOCK), f32),
             pltpu.VMEM((3, 2, CZ, CY), f32),
             pltpu.VMEM((blocks * 16, BLOCK), f32),
             pltpu.VMEM((3, points), f32),
             pltpu.VMEM((9, points), f32),
-            pltpu.SemaphoreType.DMA((4,)),
+            pltpu.SMEM(block_tile.shape, jnp.int32),
+            pltpu.SemaphoreType.DMA((4 + 2 * (blocks // CHUNK),)),
         ],
         compiler_params=params,
         cost_estimate=cost(4),
         name="collect",
-    )(place, block_tile, above, below, point_frac, cell_offset, grid, speed, grid_velocity)
+    )(pltpu.with_memory_space_constraint(block_tile, pltpu.HBM), above, below, point_frac, cell_offset, grid, inner, matrix, spread)
     return (new_velocity, new_affine, new_stress, grid_velocity.transpose(0, 1, 3, 2))
 
 

time: 32.7 us -> 29.5 us (0.902)
  Pallas kernels: 14.7 us -> 9.64 us
  waiting for transfers between devices: 9.26 us -> 11.2 us
    pallas_call x2, Pallas kernels: 8.07 us -> 4.25 us  [the longest x1 3.24 us: shards(): pl.pallas_call(lambda *refs: collect_kernel(blocks, *refs), out_shape=(sp...]
    ppermute x6, waiting for transfers between devices: 9.26 us -> 11.2 us  [exchange(): return (lax.ppermute(low, axis, down), lax.ppermute(high, axis, up))]
    pallas_call x1, Pallas kernels: 5.58 us -> 4.37 us  [shards(): pl.pallas_call(lambda *refs: deposit_kernel(blocks, *refs), out_shape=(ja...]
  transfers between devices with their start and end apart: 6 -> 6, of which waited for: 5 -> 6; matrix products, arithmetic and copies ran while one was open for 0% -> 0% of each run, Pallas kernels for 11% -> 6%
where the time goes in v1:
time: 29.5 us; the launch traced here: 29.3 us
  waiting for transfers between devices  11.2 us (38%)
  Pallas kernels  9.64 us (33%)
  starting transfers between devices  7.77 us (26%)
  between operations  0.7 us (2%)
    ppermute x6, waiting for transfers between devices, exchange(): return (lax.ppermute(low, axis, down), lax.ppermute(high, axis, up))  11.2 us
    ppermute x6, starting transfers between devices, exchange(): return (lax.ppermute(low, axis, down), lax.ppermute(high, axis, up))  7.77 us
    pallas_call x1, Pallas kernels, shards(): pl.pallas_call(lambda *refs: deposit_kernel(blocks, *refs), out_shape=(ja...  4.37 us
    pallas_call x1, Pallas kernels, shards(): pl.pallas_call(lambda *refs: collect_kernel(blocks, *refs), out_shape=(sp...  3.24 us
    pallas_call x1, Pallas kernels, shards(): pl.pallas_call(settle_kernel, out_shape=(spread_shape, out_shape, jax.Sha...  1.01 us
    pallas_call x1, Pallas kernels, shards(): pl.pallas_call(join_y_rest, out_shape=grid_shape, in_specs=[vmem] * 3, ou...  0.62 us
  transfers between devices with their start and end apart: 6, of which 6 were waited for; matrix products, arithmetic and copies ran while one was open for 0% of the time, Pallas kernels for 6%

profile of v1, /device:TPU:0, one launch (start us, length us, event | category | flops | bytes accessed | tf_op | source)
XLA Modules:
  0.0 29.3 jit_solution(9334339425716184724)
XLA Ops:
  0.6 4.4 %deposit.1 = (f32[6,4096]{1,0:T(8,128)}, f32[2480,128]{1,0:T(8,128)S(1)}, f32[40,128]{1,0:T(8,128)S(1)}, f32[40,128]{1,0:T(8,128)S(1)}) custom-call(s32[32]{0:T(128)} %refs_0_.3, s32[32]{0:T(128)} %refs_1_.1, f32[3,4096]{1,0:T(4,128)} %refs_3_.3, s32[3,4096]{1,0:T(4,128)} %refs_4_.3, f32[3,4096]{1,0:T(4,128)} %refs_4_.2, f32[9,4096]{1,0:T(8,128)} %refs_5_.1, ...), custom_call_target="tpu_custom_call" | custom-call | flops 40000000 | bytes 1000 | tf_op jit(solution)/shard_map/deposit/pallas_call | solution.py:709
  5.0 5.1 %collective-permute-start = (f32[40,128]{1,0:T(8,128)S(1)}, f32[40,128]{1,0:T(8,128)S(1)}, u32[]{:S(2)}, u32[]{:S(2)}) collective-permute-start(f32[40,128]{1,0:T(8,128)S(1)} %get-tuple-element.20), channel_id=1, source_target_pairs={{4,0},{8,4},{12,8},{0,12},{5,1},{9,5},{13,9},{1,13},{6,2},{10,6},{... | collective-permute-start | bytes 61448 | tf_op jit(solution)/shard_map/ppermute | solution.py:668
  10.1 0.0 collective-permute-start.1
  10.1 1.5 %collective-permute-done.above_ref = f32[40,128]{1,0:T(8,128)S(1)} collective-permute-done((f32[40,128]{1,0:T(8,128)S(1)}, f32[40,128]{1,0:T(8,128)S(1)}, u32[]{:S(2)}, u32[]{:S(2)}) %collective-permute-start) | collective-permute-done | bytes 20512 | tf_op jit(solution)/shard_map/ppermute | solution.py:668
  11.6 4.1 %collective-permute-done.1.below_ref = f32[40,128]{1,0:T(8,128)S(1)} collective-permute-done((f32[40,128]{1,0:T(8,128)S(1)}, f32[40,128]{1,0:T(8,128)S(1)}, u32[]{:S(2)}, u32[]{:S(2)}) %collective-permute-start.1) | collective-permute-done | bytes 20512 | tf_op jit(solution)/shard_map/ppermute | solution.py:668
  15.7 0.2 join_y_faces.1
  15.9 0.1 collective-permute-start.2
  16.0 0.5 %collective-permute-start.3 = (f32[80,128]{1,0:T(8,128)S(1)}, f32[80,128]{1,0:T(8,128)S(1)}, u32[]{:S(2)}, u32[]{:S(2)}) collective-permute-start(f32[80,128]{1,0:T(8,128)S(1)} %get-tuple-element.24), channel_id=1, source_target_pairs={{0,1},{1,2},{2,3},{3,0},{4,5},{5,6},{6,7},{7,4},{8,9},{9,10},{10,1... | collective-permute-start | bytes 122888 | tf_op jit(solution)/shard_map/ppermute | solution.py:668
  16.5 0.6 %join_y_rest.1._ = f32[2480,128]{1,0:T(8,128)S(1)} custom-call(f32[40,128]{1,0:T(8,128)S(1)} %collective-permute-done.above_ref, f32[40,128]{1,0:T(8,128)S(1)} %collective-permute-done.1.below_ref, f32[2480,128]{1,0:T(8,128)S(1)} %get-tuple-element.25._), custom_call_target="tpu_custom_call", output_to_operand_aliasing={{}: (2, {})} | custom-call | flops 8000000 | bytes 1000 | tf_op jit(solution)/shard_map/join_y_rest/pallas_call | solution.py:744
  17.1 0.0 copy-start
  17.1 0.0 copy-start.1
  17.2 0.5 %collective-permute-done.2.above_ref = f32[80,128]{1,0:T(8,128)S(1)} collective-permute-done((f32[80,128]{1,0:T(8,128)S(1)}, f32[80,128]{1,0:T(8,128)S(1)}, u32[]{:S(2)}, u32[]{:S(2)}) %collective-permute-start.2) | collective-permute-done | bytes 40992 | tf_op jit(solution)/shard_map/ppermute | solution.py:668
  17.7 2.2 %collective-permute-done.3.below_ref = f32[80,128]{1,0:T(8,128)S(1)} collective-permute-done((f32[80,128]{1,0:T(8,128)S(1)}, f32[80,128]{1,0:T(8,128)S(1)}, u32[]{:S(2)}, u32[]{:S(2)}) %collective-permute-start.3) | collective-permute-done | bytes 40992 | tf_op jit(solution)/shard_map/ppermute | solution.py:668
  19.9 0.2 join_z.1
  20.1 1.6 %collective-permute-start.4 = (f32[144,128]{1,0:T(8,128)S(1)}, f32[144,128]{1,0:T(8,128)S(1)}, u32[]{:S(2)}, u32[]{:S(2)}) collective-permute-start(f32[144,128]{1,0:T(8,128)S(1)} %get-tuple-element.26), channel_id=1, source_target_pairs={{16,0},{0,16},{17,1},{1,17},{18,2},{2,18},{19,3},{3,19},{20,4},{4,... | collective-permute-start | bytes 221192 | tf_op jit(solution)/shard_map/ppermute | solution.py:668
  21.7 0.5 %collective-permute-start.5 = (f32[144,128]{1,0:T(8,128)S(1)}, f32[144,128]{1,0:T(8,128)S(1)}, u32[]{:S(2)}, u32[]{:S(2)}) collective-permute-start(f32[144,128]{1,0:T(8,128)S(1)} %get-tuple-element.27), channel_id=1, source_target_pairs={{0,16},{16,0},{1,17},{17,1},{2,18},{18,2},{3,19},{19,3},{4,20},{20... | collective-permute-start | bytes 221192 | tf_op jit(solution)/shard_map/ppermute | solution.py:668
  22.2 1.0 %settle.1 = (f32[4896,128]{1,0:T(8,128)S(1)}, f32[3,16,32,64]{3,2,1,0:T(8,128)S(1)}, bf16[256,256]{1,0:T(8,128)(2,1)S(1)}) custom-call(f32[2480,128]{1,0:T(8,128)S(1)} %get-tuple-element.28.grid_ref.refs_5_), custom_call_target="tpu_custom_call" | custom-call | flops 16000000 | bytes 1000 | tf_op jit(solution)/shard_map/settle/pallas_call | solution.py:767
  23.2 1.7 %collective-permute-done.4.refs_1_ = f32[144,128]{1,0:T(8,128)S(1)} collective-permute-done((f32[144,128]{1,0:T(8,128)S(1)}, f32[144,128]{1,0:T(8,128)S(1)}, u32[]{:S(2)}, u32[]{:S(2)}) %collective-permute-start.4) | collective-permute-done | bytes 73760 | tf_op jit(solution)/shard_map/ppermute | solution.py:668
  24.9 1.2 %collective-permute-done.5.refs_2_ = f32[144,128]{1,0:T(8,128)S(1)} collective-permute-done((f32[144,128]{1,0:T(8,128)S(1)}, f32[144,128]{1,0:T(8,128)S(1)}, u32[]{:S(2)}, u32[]{:S(2)}) %collective-permute-start.5) | collective-permute-done | bytes 73760 | tf_op jit(solution)/shard_map/ppermute | solution.py:668
  26.1 0.0 copy-done
  26.1 0.0 copy-done.1
  26.1 3.2 %collect.1 = (f32[4896,128]{1,0:T(8,128)S(1)}, f32[3,16,32,64]{3,2,1,0:T(8,128)}, f32[3,4096]{1,0:T(4,128)}, f32[9,4096]{1,0:T(8,128)}) custom-call(s32[32]{0:T(128)} %refs_0_.3, f32[144,128]{1,0:T(8,128)S(1)} %collective-permute-done.4.refs_1_, f32[144,128]{1,0:T(8,128)S(1)} %collective-permute-done.5.refs_2_, ...), custom_call_target="tpu_custom_call", output_to_operand_aliasing={{0}: (8, {})} | custom-call | flops 32000000 | bytes 1000 | tf_op jit(solution)/shard_map/collect/pallas_call | solution.py:781
Async XLA Ops:
  5.0 6.6 %collective-permute-start = (f32[40,128]{1,0:T(8,128)S(1)}, f32[40,128]{1,0:T(8,128)S(1)}, u32[]{:S(2)}, u32[]{:S(2)}) collective-permute-start(f32[40,128]{1,0:T(8,128)S(1)} %get-tuple-element.20), channel_id=1, source_target_pairs={{4,0},{8,4},{12,8},{0,12},{5,1},{9,5},{13,9},{1,13},{6,2},{10,6},{... | collective-permute-start | bytes 61448 | tf_op jit(solution)/shard_map/ppermute | solution.py:668
  10.1 5.6 %collective-permute-start.1 = (f32[40,128]{1,0:T(8,128)S(1)}, f32[40,128]{1,0:T(8,128)S(1)}, u32[]{:S(2)}, u32[]{:S(2)}) collective-permute-start(f32[40,128]{1,0:T(8,128)S(1)} %get-tuple-element.21), channel_id=1, source_target_pairs={{0,4},{4,8},{8,12},{12,0},{1,5},{5,9},{9,13},{13,1},{2,6},{6,10},{... | collective-permute-start | bytes 61448 | tf_op jit(solution)/shard_map/ppermute | solution.py:668
  15.9 1.7 %collective-permute-start.2 = (f32[80,128]{1,0:T(8,128)S(1)}, f32[80,128]{1,0:T(8,128)S(1)}, u32[]{:S(2)}, u32[]{:S(2)}) collective-permute-start(f32[80,128]{1,0:T(8,128)S(1)} %get-tuple-element.23), channel_id=1, source_target_pairs={{1,0},{2,1},{3,2},{0,3},{5,4},{6,5},{7,6},{4,7},{9,8},{10,9},{11,1... | collective-permute-start | bytes 122888 | tf_op jit(solution)/shard_map/ppermute | solution.py:668
  16.0 3.9 %collective-permute-start.3 = (f32[80,128]{1,0:T(8,128)S(1)}, f32[80,128]{1,0:T(8,128)S(1)}, u32[]{:S(2)}, u32[]{:S(2)}) collective-permute-start(f32[80,128]{1,0:T(8,128)S(1)} %get-tuple-element.24), channel_id=1, source_target_pairs={{0,1},{1,2},{2,3},{3,0},{4,5},{5,6},{6,7},{7,4},{8,9},{9,10},{10,1... | collective-permute-start | bytes 122888 | tf_op jit(solution)/shard_map/ppermute | solution.py:668
  17.1 9.0 %copy-start = (f32[3,4096]{1,0:T(4,128)S(1)}, f32[3,4096]{1,0:T(4,128)}, u32[]{:S(2)}) copy-start(f32[3,4096]{1,0:T(4,128)} %refs_3_.3) | copy-start | bytes 147460
  17.1 9.0 %copy-start.1 = (s32[3,4096]{1,0:T(4,128)S(1)}, s32[3,4096]{1,0:T(4,128)}, u32[]{:S(2)}) copy-start(s32[3,4096]{1,0:T(4,128)} %refs_4_.3) | copy-start | bytes 147460
  20.1 4.8 %collective-permute-start.4 = (f32[144,128]{1,0:T(8,128)S(1)}, f32[144,128]{1,0:T(8,128)S(1)}, u32[]{:S(2)}, u32[]{:S(2)}) collective-permute-start(f32[144,128]{1,0:T(8,128)S(1)} %get-tuple-element.26), channel_id=1, source_target_pairs={{16,0},{0,16},{17,1},{1,17},{18,2},{2,18},{19,3},{3,19},{20,4},{4,... | collective-permute-start | bytes 221192 | tf_op jit(solution)/shard_map/ppermute | solution.py:668
  21.7 4.4 %collective-permute-start.5 = (f32[144,128]{1,0:T(8,128)S(1)}, f32[144,128]{1,0:T(8,128)S(1)}, u32[]{:S(2)}, u32[]{:S(2)}) collective-permute-start(f32[144,128]{1,0:T(8,128)S(1)} %get-tuple-element.27), channel_id=1, source_target_pairs={{0,16},{16,0},{1,17},{17,1},{2,18},{18,2},{3,19},{19,3},{4,20},{20... | collective-permute-start | bytes 221192 | tf_op jit(solution)/shard_map/ppermute | solution.py:668

commit v2 on v1

--- a/solution.py
+++ b/solution.py
@@ -4,6 +4,7 @@
 from jax.experimental import pallas as pl
 from jax.experimental.pallas import tpu as pltpu
 from jax.sharding import PartitionSpec as P
+
 
 CX = 16
 CY = 64
@@ -37,6 +38,9 @@
 REST = 2 * PY - 128
 STRIDE = 40
 CHUNK = 16
+PARTS = 18
+SEATS = BLOCK // PARTS
+SPREADS = -(-(CY // 4) // SEATS)
 VMEM_LIMIT = 16 * 1024 * 1024
 FAR = 3.0e38
 
@@ -170,10 +174,13 @@
 
 
 def expansion():
-    row = lax.broadcasted_iota(jnp.int32, (2 * BLOCK, 2 * BLOCK), 0)
-    col = lax.broadcasted_iota(jnp.int32, (2 * BLOCK, 2 * BLOCK), 1)
-    source = (col // 16) * 4 + col % 8 + jnp.where(col % 16 < 8, 0, BLOCK)
-    return jnp.where(row == source, 1.0, 0.0).astype(jnp.bfloat16)
+    row = lax.broadcasted_iota(jnp.int32, (2 * BLOCK, SPREADS * BLOCK), 0)
+    col = lax.broadcasted_iota(jnp.int32, (2 * BLOCK, SPREADS * BLOCK), 1)
+    tile = (col // BLOCK) * SEATS + (col % BLOCK) // PARTS
+    part = (col % BLOCK) % PARTS
+    source = 4 * tile + part % 6 + jnp.where(part // 6 == 1, BLOCK, 0)
+    seated = (col % BLOCK < SEATS * PARTS) & (tile < CY // 4)
+    return jnp.where((row == source) & seated, 1.0, 0.0).astype(jnp.bfloat16)
 
 
 def expand(values, matrix, spread_ref, row):
@@ -181,8 +188,9 @@
         jnp.concatenate(split(values), axis=1), matrix, preferred_element_type=jnp.float32
     )
     count = values.shape[0]
-    spread_ref[pl.ds(pl.multiple_of(row, 8), count), :] = wide[:, 0:BLOCK]
-    spread_ref[pl.ds(pl.multiple_of(row + PX * PLANE, 8), count), :] = wide[:, BLOCK:]
+    for spread in range(SPREADS):
+        rows = pl.ds(pl.multiple_of(row + spread * PX * PLANE, 8), count)
+        spread_ref[rows, :] = wide[:, spread * BLOCK : (spread + 1) * BLOCK]
 
 
 def window_rows(corner, step):
@@ -197,21 +205,21 @@
     return pltpu.roll(values, shift % 128, 1) if shift % 128 else values
 
 
-def pack_pairs(first, second, target):
+def pack_pairs(first, second, target, start=0):
     lane = lane_index()
     last = jnp.zeros((8, BLOCK), jnp.float32)
     for spot, (one, two) in enumerate(zip(first, second)):
-        target[8 * spot : 8 * spot + 8, :] = jnp.where(lane < PY, one, roll(two, PY))
+        target[tile_rows(start + spot), :] = jnp.where(lane < PY, one, roll(two, PY))
         last = jnp.where(lane // REST == spot, roll(two, REST * spot - (PY - REST)), last)
-    target[8 * len(first) : 8 * len(first) + 8, :] = last
-
-
-def unpack_pairs(source, count):
+    target[tile_rows(start + len(first)), :] = last
+
+
+def unpack_pairs(source, count, start=0):
     lane = lane_index()
-    last = source[8 * count : 8 * count + 8, :]
+    last = source[tile_rows(start + count), :]
     first, second = [], []
     for spot in range(count):
-        tile = source[8 * spot : 8 * spot + 8, :]
+        tile = source[tile_rows(start + spot), :]
         first.append(jnp.where(lane < PY, tile, 0.0))
         tail = jnp.where(lane < PY, roll(last, (PY - REST) - REST * spot), 0.0)
         second.append(jnp.where(lane < PY - REST, roll(tile, -PY), tail))
@@ -236,6 +244,7 @@
     grid_ref,
     low_ref,
     high_ref,
+    early_ref,
     tile_ref,
     count_ref,
     frac_ref,
@@ -381,6 +390,12 @@
     for spot in range(SPAN):
         low_ref[tile_rows(spot), :] = low[spot]
         high_ref[tile_rows(spot), :] = high[spot]
+    for side, start in enumerate((0, CX)):
+        planes = [
+            [grid_ref[tile_rows((start + part) * FACE + spot), :] for spot in range(FACE)]
+            for part in range(2)
+        ]
+        pack_pairs(planes[0], planes[1], early_ref, side * (FACE + 1))
     stress_copy.wait()
 
 
@@ -395,6 +410,9 @@
 
 
 FACE = PLANE // 8
+
+
+RIM_TILES = [(part, spot) for part in range(2) for spot in range(1, FACE - 1)]
 
 
 def join_y_faces(above_ref, below_ref, _, grid_ref, low_ref, high_ref):
@@ -415,18 +433,48 @@
     add_y(grid_ref, above, below, tiles)
 
 
-def join_z(above_ref, below_ref, _, grid_ref, low_ref, high_ref):
+def join_z(above_ref, below_ref, _, grid_ref, late_ref):
     half = PX // 2
     for source, side in ((below_ref, 0), (above_ref, FACE - 1)):
         first, second = unpack_pairs(source, half)
         for step, value in enumerate(first + second):
             grid_ref[tile_rows(step * FACE + side), :] += value
-    for target, start in ((low_ref, 0), (high_ref, CX)):
-        planes = [
-            [grid_ref[tile_rows((start + part) * FACE + spot), :] for spot in range(FACE)]
-            for part in range(2)
-        ]
-        pack_pairs(planes[0], planes[1], target)
+    lane = lane_index()
+    for place, start in enumerate((0, CX)):
+
+        def tile(part, spot):
+            return grid_ref[tile_rows((start + part) * FACE + spot), :]
+
+        rim = jnp.zeros((8, BLOCK), jnp.float32)
+        for seat, (part, spot) in enumerate(RIM_TILES):
+            rim = jnp.where(lane // 2 % 32 == seat, roll(tile(part, spot), 2 * seat), rim)
+        for side, spot in enumerate((0, FACE - 1)):
+            one, two = tile(0, spot), tile(1, spot)
+            tail = lane // REST == 15 + 16 * side
+            rim = jnp.where(tail, roll(two, 64 * side - 2), rim)
+            late_ref[tile_rows(3 * place + 1 + side), :] = jnp.where(
+                lane < PY, one, roll(two, PY)
+            )
+        late_ref[tile_rows(3 * place), :] = rim
+
+
+def rim_lanes(lane):
+    return (lane // 2) % (CY // 2) == 0
+
+
+def late_planes(source, start):
+    lane = lane_index()
+    mask = rim_lanes(lane) & (lane < PY)
+    rim = source[tile_rows(start), :]
+    planes = [[None] * FACE for _ in range(2)]
+    for seat, (part, spot) in enumerate(RIM_TILES):
+        planes[part][spot] = jnp.where(mask, roll(rim, -2 * seat), 0.0)
+    for side, spot in enumerate((0, FACE - 1)):
+        tile = source[tile_rows(start + 1 + side), :]
+        tail = jnp.where(lane < PY, roll(rim, 2 - 64 * side), 0.0)
+        planes[0][spot] = jnp.where(lane < PY, tile, 0.0)
+        planes[1][spot] = jnp.where(lane < PY - REST, roll(tile, -PY), tail)
+    return planes
 
 
 def place_bounds():
@@ -498,7 +546,18 @@
             u_ref[pl.ds(start, count, stride=PLANE), :] = values[channel]
 
 
-def settle_kernel(grid_ref, spread_ref, out_ref, matrix_ref, u_ref):
+def settle_kernel(
+    source_ref, grid_ref, spread_ref, out_ref, matrix_ref, edge_ref, u_ref
+):
+    rim = rim_lanes(lane_index())
+    for side, start, place in ((1, 0, 0), (0, CX, 2)):
+        for part, tiles in enumerate(unpack_pairs(source_ref, FACE, side * (FACE + 1))):
+            for spot, value in enumerate(tiles):
+                mine = grid_ref[tile_rows((start + part) * FACE + spot), :]
+                if 0 < spot < FACE - 1:
+                    mine = mine + jnp.where(rim, 0.0, value)
+                edge_ref[tile_rows((place + part) * FACE + spot), :] = mine
+
     def plane(step, carry):
         row = pl.multiple_of(step * PLANE, 8)
         settle_plane(grid_ref, row, u_ref, step, out_ref, step - 1)
@@ -518,14 +577,41 @@
     lax.fori_loop(2, CX, spread, 0, unroll=7)
 
 
+def weights_kernel(blocks, frac_ref, offset_ref, x_ref, z_ref, y_ref):
+    for block in range(blocks):
+        lanes = slice(block * BLOCK, (block + 1) * BLOCK)
+        fraction, offset = point_rows(frac_ref, offset_ref, lanes)
+        for side, values in enumerate(lane_weights(fraction[0], offset[0])):
+            x_ref[tile_rows(2 * block + side), :] = values
+        weight_z, first_z = pair_weights(fraction[2], offset[2])
+        for spot, values in enumerate(weight_z + first_z):
+            z_ref[tile_rows(6 * block + spot), :] = values
+        plain, moment = spline(fraction[1])
+        slot = lax.broadcasted_iota(jnp.int32, (8, BLOCK), 0)
+        pieces = []
+        for group in range(3):
+            row = slot + 8 * group
+            masks = slot_masks(jnp.where(row < PARTS, row % 6, -100), offset[1])
+            values = jnp.concatenate([pick(masks, plain), pick(masks, moment)], axis=1)
+            high, low = split(values)
+            wide = lax.broadcasted_iota(jnp.int32, values.shape, 0) + 8 * group
+            pieces.append(
+                jnp.where(wide < 12, high.astype(jnp.float32), low.astype(jnp.float32))
+            )
+        pieces.append(jnp.zeros_like(pieces[0]))
+        y_ref[32 * block : 32 * block + 32, :] = jnp.concatenate(pieces, axis=0).astype(
+            jnp.bfloat16
+        )
+
+
 def collect_kernel(
     blocks,
-    tile_hbm,
-    above_ref,
-    below_ref,
-    frac_ref,
-    offset_ref,
-    grid_ref,
+    tile_vmem,
+    late_ref,
+    x_ref,
+    z_ref,
+    y_ref,
+    early_ref,
     inner_ref,
     matrix_ref,
     _,
@@ -542,18 +628,17 @@
     tile_ref,
     sems,
 ):
-    tile_copy = pltpu.make_async_copy(tile_hbm, tile_ref, sems.at[3 + 2 * (blocks // CHUNK)])
+    tile_copy = pltpu.make_async_copy(tile_vmem, tile_ref, sems.at[3 + 2 * (blocks // CHUNK)])
     tile_copy.start()
     inner = pltpu.make_async_copy(
         inner_ref.at[:, pl.ds(1, CX - 2)], out_hbm.at[:, pl.ds(1, CX - 2)], sems.at[2]
     )
     inner.start()
-    for source, start, spot in ((below_ref, 0, 0), (above_ref, CX, 2)):
-        first, second = unpack_pairs(source, FACE)
-        for tile, value in enumerate(first + second):
-            edge_ref[tile_rows(spot * FACE + tile), :] = (
-                grid_ref[tile_rows(start * FACE + tile), :] + value
-            )
+    for side, place in ((1, 0), (0, 2)):
+        for part, tiles in enumerate(late_planes(late_ref, 3 * side)):
+            for spot, value in enumerate(tiles):
+                rows = tile_rows((place + part) * FACE + spot)
+                edge_ref[rows, :] = early_ref[rows, :] + value
     for spot, step in enumerate((0, 1, CX, CX + 1)):
         out_step = {1: 0, CX: 1}.get(step)
         settle_plane(edge_ref, spot * PLANE, u_ref, step, out_ref, out_step, spot)
@@ -578,31 +663,28 @@
     def one_block(block):
         lanes = pl.ds(pl.multiple_of(block * BLOCK, BLOCK), BLOCK)
         corner, corner_y = tile_corner(tile_ref[block])
-        fraction, offset = point_rows(frac_ref, offset_ref, lanes)
-        weight_x, first_x = x_weights(fraction[0], offset[0])
-        weight_z, first_z = pair_weights(fraction[2], offset[2])
-        weight_y, first_y = lane_weights(fraction[1], offset[1])
-        right_high, right_low = split(jnp.concatenate([weight_y, first_y], axis=1))
-        right_high = right_high.astype(jnp.float32)
-        fill = jnp.zeros((BLOCK - 16, 2 * BLOCK), jnp.float32)
-        right_one = jnp.concatenate([right_high, right_high, fill], axis=0)
-        right_two = jnp.concatenate(
-            [right_low.astype(jnp.float32), jnp.zeros_like(right_high), fill], axis=0
-        )
-        half = corner_y // 32
-        corner = corner + half * (PX * PLANE)
-        turn = (128 - 4 * (corner_y - 32 * half)) & 127
+
+        def x_row(slot):
+            return x_ref[pl.ds(block * 16 + slot, 8, stride=0), :]
+
+        def z_tile(slot):
+            return z_ref[pl.ds(pl.multiple_of(block * 48 + 8 * slot, 8), 8), :]
+
+        weight_x = [x_row(slot) for slot in range(6)]
+        first_x = [x_row(8 + slot) for slot in range(6)]
+        weight_z = [z_tile(slot) for slot in range(3)]
+        first_z = [z_tile(3 + slot) for slot in range(3)]
+        right = y_ref[pl.ds(pl.multiple_of(block * 32, 32), 32), :]
+        seat = corner_y // 4
+        spread = seat // SEATS
+        corner = corner + spread * (PX * PLANE)
+        turn = (128 - PARTS * (seat - spread * SEATS)) & 127
         left = jnp.concatenate(
             [pltpu.roll(spread_ref[window_rows(corner, step), :], turn, 1) for step in range(6)],
             axis=0,
         ).astype(jnp.bfloat16)
 
-        def dot(right):
-            return jnp.dot(
-                left, right.astype(jnp.bfloat16), preferred_element_type=jnp.float32
-            )
-
-        sums = dot(right_one) + dot(right_two)
+        sums = jnp.dot(left[:, 0:24], right[0:24], preferred_element_type=jnp.float32)
 
         def over_x(weights, column):
             result = []
@@ -665,10 +747,19 @@
     count = lax.axis_size(axis)
     up = [(i, (i + 1) % count) for i in range(count)]
     down = [(target, source) for source, target in up]
-    return lax.ppermute(low, axis, down), lax.ppermute(high, axis, up)
-
-
-def shards(
+    above = lax.ppermute(low, axis, down)
+    below = lax.ppermute(high, axis, up)
+    return above, below
+
+
+def exchange_both(message, axis):
+    if lax.axis_size(axis) == 2:
+        return lax.ppermute(message, axis, [(0, 1), (1, 0)])
+    half = message.shape[0] // 2
+    return jnp.concatenate(exchange(message[:half], message[half:], axis))
+
+
+def step(
     point_frac,
     cell_offset,
     point_velocity,
@@ -706,16 +797,17 @@
         point_stress,
         mass,
     )
-    new_stress, grid, low, high = pl.pallas_call(
+    new_stress, grid, low, high, early = pl.pallas_call(
         lambda *refs: deposit_kernel(blocks, *refs),
         out_shape=(
             jax.ShapeDtypeStruct((6, points), f32),
             grid_shape,
             message(SPAN),
             message(SPAN),
+            message(2 * (FACE + 1)),
         ),
         in_specs=[hbm] * 8,
-        out_specs=(hbm, vmem, vmem, vmem),
+        out_specs=(hbm,) + (vmem,) * 4,
         scratch_shapes=[
             pltpu.SMEM(block_tile.shape, jnp.int32),
             pltpu.SMEM(block_count.shape, jnp.int32),
@@ -730,7 +822,22 @@
         cost_estimate=cost(5),
         name="deposit",
     )(*[pltpu.with_memory_space_constraint(array, pltpu.HBM) for array in inputs])
+    weigh = pl.pallas_call(
+        lambda *refs: weights_kernel(blocks, *refs),
+        out_shape=(
+            message(2 * blocks),
+            message(6 * blocks),
+            jax.ShapeDtypeStruct((32 * blocks, 2 * BLOCK), jnp.bfloat16),
+        ),
+        in_specs=[vmem] * 2,
+        out_specs=(vmem,) * 3,
+        compiler_params=params,
+        cost_estimate=cost(1),
+        name="weights",
+    )
+    weights = weigh(point_frac, cell_offset)
     above, below = exchange(low, high, "gy")
+    early = exchange_both(early, "gx")
     grid, low, high = pl.pallas_call(
         join_y_faces,
         out_shape=(grid_shape, message(PX // 2 + 1), message(PX // 2 + 1)),
@@ -752,32 +859,33 @@
         name="join_y_rest",
     )(above, below, grid)
     above, below = exchange(low, high, "gz")
-    grid, low, high = pl.pallas_call(
+    grid, late = pl.pallas_call(
         join_z,
-        out_shape=(grid_shape, message(FACE + 1), message(FACE + 1)),
+        out_shape=(grid_shape, message(6)),
         in_specs=[vmem] * 3,
-        out_specs=(vmem,) * 3,
+        out_specs=(vmem,) * 2,
         input_output_aliases={2: 0},
         compiler_params=params,
         cost_estimate=cost(0.3),
         name="join_z",
     )(above, below, grid)
-    above, below = exchange(low, high, "gx")
-    spread_shape = message(2 * TILES)
-    spread, inner, matrix = pl.pallas_call(
+    late = exchange_both(late, "gx")
+    spread_shape = message(SPREADS * TILES)
+    spread, inner, matrix, edge = pl.pallas_call(
         settle_kernel,
         out_shape=(
             spread_shape,
             out_shape,
-            jax.ShapeDtypeStruct((2 * BLOCK, 2 * BLOCK), jnp.bfloat16),
+            jax.ShapeDtypeStruct((2 * BLOCK, SPREADS * BLOCK), jnp.bfloat16),
+            message(4 * FACE),
         ),
-        in_specs=[vmem],
-        out_specs=(vmem, vmem, vmem),
+        in_specs=[vmem] * 2,
+        out_specs=(vmem,) * 4,
         scratch_shapes=[pltpu.VMEM((PX * PLANE, BLOCK), f32)],
         compiler_params=params,
         cost_estimate=cost(2),
         name="settle",
-    )(grid)
+    )(early, grid)
     _, grid_velocity, new_velocity, new_affine = pl.pallas_call(
         lambda *refs: collect_kernel(blocks, *refs),
         out_shape=(
@@ -786,7 +894,7 @@
             jax.ShapeDtypeStruct((3, points), f32),
             jax.ShapeDtypeStruct((9, points), f32),
         ),
-        in_specs=[hbm] + [vmem] * 8,
+        in_specs=[vmem] * 9,
         out_specs=(vmem, hbm, hbm, hbm),
         input_output_aliases={8: 0},
         scratch_shapes=[
@@ -802,14 +910,14 @@
         compiler_params=params,
         cost_estimate=cost(4),
         name="collect",
-    )(pltpu.with_memory_space_constraint(block_tile, pltpu.HBM), above, below, point_frac, cell_offset, grid, inner, matrix, spread)
+    )(block_tile, late, *weights, edge, inner, matrix, spread)
     return (new_velocity, new_affine, new_stress, grid_velocity.transpose(0, 1, 3, 2))
 
 
 def solution(mesh):
     points = ("gx", "gy", "gz")
     return jax.shard_map(
-        shards,
+        step,
         mesh=mesh,
         in_specs=(P(None, points),) * 5 + (P(points),) * 3,
         out_specs=(P(None, points),) * 3 + (P(None, "gx", "gy", "gz"),),

time: 29.5 us -> 28.7 us (0.973)
  waiting for transfers between devices: 11.2 us -> 9.64 us
  Pallas kernels: 9.64 us -> 10.3 us
    ppermute x6, waiting for transfers between devices: 11.2 us -> 9.64 us  [the longest x2 6.34 us: exchange(): below = lax.ppermute(high, axis, up)]
    pallas_call x6 -> x7, Pallas kernels: 9.64 us -> 10.3 us  [the longest x1 4.51 us: step(): pl.pallas_call(lambda *refs: deposit_kernel(blocks, *refs), out_shape=(ja...]
  transfers between devices with their start and end apart: 6 -> 6, of which waited for: 6 -> 5; matrix products, arithmetic and copies ran while one was open for 0% -> 0% of each run, Pallas kernels for 6% -> 10%
where the time goes in v2:
time: 28.7 us; the launch traced here: 28.5 us
  Pallas kernels  10.3 us (36%)
  waiting for transfers between devices  9.64 us (34%)
  starting transfers between devices  7.79 us (27%)
  between operations  0.72 us (3%)
    ppermute x2, waiting for transfers between devices, exchange(): below = lax.ppermute(high, axis, up)  6.34 us
    pallas_call x1, Pallas kernels, step(): pl.pallas_call(lambda *refs: deposit_kernel(blocks, *refs), out_shape=(ja...  4.51 us
    ppermute x2, starting transfers between devices, exchange(): above = lax.ppermute(low, axis, down)  3.67 us
    ppermute x2, starting transfers between devices, exchange_both(): return lax.ppermute(message, axis, [(0, 1), (1, 0)])  3.62 us
    pallas_call x1, Pallas kernels, step(): pl.pallas_call(lambda *refs: collect_kernel(blocks, *refs), out_shape=(sp...  2.86 us
    ppermute x2, waiting for transfers between devices, exchange(): above = lax.ppermute(low, axis, down)  1.98 us
    pallas_call x1, Pallas kernels, step(): pl.pallas_call(settle_kernel, out_shape=(spread_shape, out_shape, jax.Sha...  1.39 us
    ppermute x2, waiting for transfers between devices, exchange_both(): return lax.ppermute(message, axis, [(0, 1), (1, 0)])  1.31 us
  transfers between devices with their start and end apart: 6, of which 5 were waited for; matrix products, arithmetic and copies ran while one was open for 0% of the time, Pallas kernels for 10%

profile of v2, /device:TPU:0, one launch (start us, length us, event | category | flops | bytes accessed | tf_op | source)
XLA Modules:
  0.0 28.5 jit_solution(15325122324926119398)
XLA Ops:
  0.6 4.5 %deposit.1 = (f32[6,4096]{1,0:T(8,128)}, f32[2480,128]{1,0:T(8,128)S(1)}, f32[40,128]{1,0:T(8,128)S(1)}, f32[40,128]{1,0:T(8,128)S(1)}, f32[288,128]{1,0:T(8,128)S(1)}) custom-call(s32[32]{0:T(128)} %refs_0_.5, s32[32]{0:T(128)} %refs_1_.2, f32[3,4096]{1,0:T(4,128)} %refs_0_.4, s32[3,4096]{1,0:T(4,128)} %refs_1_.3, f32[3,4096]{1,0:T(4,128)} %refs_4_.1, ...), custom_call_target="tpu_custom_call" | custom-call | flops 40000000 | bytes 1000 | tf_op jit(solution)/shard_map/deposit/pallas_call | solution.py:800
  5.2 3.0 %collective-permute-start.5 = (f32[288,128]{1,0:T(8,128)S(1)}, f32[288,128]{1,0:T(8,128)S(1)}, u32[]{:S(2)}, u32[]{:S(2)}) collective-permute-start(f32[288,128]{1,0:T(8,128)S(1)} %get-tuple-element.34), channel_id=1, source_target_pairs={{0,16},{16,0},{1,17},{17,1},{2,18},{18,2},{3,19},{19,3},{4,20},{20... | collective-permute-start | bytes 442376 | tf_op jit(solution)/shard_map/ppermute | solution.py:757
  8.2 3.6 %collective-permute-start = (f32[40,128]{1,0:T(8,128)S(1)}, f32[40,128]{1,0:T(8,128)S(1)}, u32[]{:S(2)}, u32[]{:S(2)}) collective-permute-start(f32[40,128]{1,0:T(8,128)S(1)} %get-tuple-element.24), channel_id=1, source_target_pairs={{4,0},{8,4},{12,8},{0,12},{5,1},{9,5},{13,9},{1,13},{6,2},{10,6},{... | collective-permute-start | bytes 61448 | tf_op jit(solution)/shard_map/ppermute | solution.py:750
  11.8 0.0 collective-permute-start.1
  11.8 1.5 %collective-permute-done.above_ref = f32[40,128]{1,0:T(8,128)S(1)} collective-permute-done((f32[40,128]{1,0:T(8,128)S(1)}, f32[40,128]{1,0:T(8,128)S(1)}, u32[]{:S(2)}, u32[]{:S(2)}) %collective-permute-start) | collective-permute-done | bytes 20512 | tf_op jit(solution)/shard_map/ppermute | solution.py:750
  13.3 4.1 %collective-permute-done.1.below_ref = f32[40,128]{1,0:T(8,128)S(1)} collective-permute-done((f32[40,128]{1,0:T(8,128)S(1)}, f32[40,128]{1,0:T(8,128)S(1)}, u32[]{:S(2)}, u32[]{:S(2)}) %collective-permute-start.1) | collective-permute-done | bytes 20512 | tf_op jit(solution)/shard_map/ppermute | solution.py:751
  17.4 0.2 join_y_faces.1
  17.6 0.1 collective-permute-start.2
  17.7 0.5 %collective-permute-start.3 = (f32[80,128]{1,0:T(8,128)S(1)}, f32[80,128]{1,0:T(8,128)S(1)}, u32[]{:S(2)}, u32[]{:S(2)}) collective-permute-start(f32[80,128]{1,0:T(8,128)S(1)} %get-tuple-element.28), channel_id=1, source_target_pairs={{0,1},{1,2},{2,3},{3,0},{4,5},{5,6},{6,7},{7,4},{8,9},{9,10},{10,1... | collective-permute-start | bytes 122888 | tf_op jit(solution)/shard_map/ppermute | solution.py:751
  18.2 0.6 %join_y_rest.1._ = f32[2480,128]{1,0:T(8,128)S(1)} custom-call(f32[40,128]{1,0:T(8,128)S(1)} %collective-permute-done.above_ref, f32[40,128]{1,0:T(8,128)S(1)} %collective-permute-done.1.below_ref, f32[2480,128]{1,0:T(8,128)S(1)} %get-tuple-element.29._), custom_call_target="tpu_custom_call", output_to_operand_aliasing={{}: (2, {})} | custom-call | flops 8000000 | bytes 1000 | tf_op jit(solution)/shard_map/join_y_rest/pallas_call | solution.py:851
  18.8 0.0 copy-start
  18.8 0.0 copy-start.1
  18.8 0.0 copy-start.2
  18.8 0.5 %collective-permute-done.2.above_ref = f32[80,128]{1,0:T(8,128)S(1)} collective-permute-done((f32[80,128]{1,0:T(8,128)S(1)}, f32[80,128]{1,0:T(8,128)S(1)}, u32[]{:S(2)}, u32[]{:S(2)}) %collective-permute-start.2) | collective-permute-done | bytes 40992 | tf_op jit(solution)/shard_map/ppermute | solution.py:750
  19.3 2.2 %collective-permute-done.3.below_ref = f32[80,128]{1,0:T(8,128)S(1)} collective-permute-done((f32[80,128]{1,0:T(8,128)S(1)}, f32[80,128]{1,0:T(8,128)S(1)}, u32[]{:S(2)}, u32[]{:S(2)}) %collective-permute-start.3) | collective-permute-done | bytes 40992 | tf_op jit(solution)/shard_map/ppermute | solution.py:751
  21.6 0.2 join_z.1
  21.8 0.6 %collective-permute-start.4 = (f32[48,128]{1,0:T(8,128)S(1)}, f32[48,128]{1,0:T(8,128)S(1)}, u32[]{:S(2)}, u32[]{:S(2)}) collective-permute-start(f32[48,128]{1,0:T(8,128)S(1)} %get-tuple-element.30), channel_id=1, source_target_pairs={{0,16},{16,0},{1,17},{17,1},{2,18},{18,2},{3,19},{19,3},{4,20},{20... | collective-permute-start | bytes 73736 | tf_op jit(solution)/shard_map/ppermute | solution.py:757
  22.3 0.0 copy-done
  22.3 0.0 copy-done.1
  22.4 0.6 %weights.1 = (f32[512,128]{1,0:T(8,128)S(1)}, f32[1536,128]{1,0:T(8,128)S(1)}, bf16[1024,256]{1,0:T(8,128)(2,1)S(1)}) custom-call(f32[3,4096]{1,0:T(4,128)S(1)} %copy-done, s32[3,4096]{1,0:T(4,128)S(1)} %copy-done.1), custom_call_target="tpu_custom_call" | custom-call | flops 8000000 | bytes 1000 | tf_op jit(solution)/shard_map/weights/pallas_call | solution.py:838
  22.9 0.0 collective-permute-done.5.source_ref
  22.9 1.4 %settle.1 = (f32[7344,128]{1,0:T(8,128)S(1)}, f32[3,16,32,64]{3,2,1,0:T(8,128)S(1)}, bf16[256,384]{1,0:T(8,128)(2,1)S(1)}, f32[544,128]{1,0:T(8,128)S(1)}) custom-call(f32[288,128]{1,0:T(8,128)S(1)} %collective-permute-done.5.source_ref, f32[2480,128]{1,0:T(8,128)S(1)} %get-tuple-element.35.grid_ref), custom_call_target="tpu_custom_call" | custom-call | flops 16000000 | bytes 1000 | tf_op jit(solution)/shard_map/settle/pallas_call | solution.py:874
  24.3 1.3 %collective-permute-done.4.refs_1_ = f32[48,128]{1,0:T(8,128)S(1)} collective-permute-done((f32[48,128]{1,0:T(8,128)S(1)}, f32[48,128]{1,0:T(8,128)S(1)}, u32[]{:S(2)}, u32[]{:S(2)}) %collective-permute-start.4) | collective-permute-done | bytes 24608 | tf_op jit(solution)/shard_map/ppermute | solution.py:757
  25.6 0.0 copy-done.2
  25.7 2.9 %collect.1 = (f32[7344,128]{1,0:T(8,128)S(1)}, f32[3,16,32,64]{3,2,1,0:T(8,128)}, f32[3,4096]{1,0:T(4,128)}, f32[9,4096]{1,0:T(8,128)}) custom-call(s32[32]{0:T(128)S(1)} %copy-done.2, f32[48,128]{1,0:T(8,128)S(1)} %collective-permute-done.4.refs_1_, f32[512,128]{1,0:T(8,128)S(1)} %get-tuple-element.31.refs_2_, ...), custom_call_target="tpu_custom_call", output_to_operand_aliasing={{0}: (8, {})} | custom-call | flops 32000000 | bytes 1000 | tf_op jit(solution)/shard_map/collect/pallas_call | solution.py:889
Async XLA Ops:
  5.2 17.8 %collective-permute-start.5 = (f32[288,128]{1,0:T(8,128)S(1)}, f32[288,128]{1,0:T(8,128)S(1)}, u32[]{:S(2)}, u32[]{:S(2)}) collective-permute-start(f32[288,128]{1,0:T(8,128)S(1)} %get-tuple-element.34), channel_id=1, source_target_pairs={{0,16},{16,0},{1,17},{17,1},{2,18},{18,2},{3,19},{19,3},{4,20},{20... | collective-permute-start | bytes 442376 | tf_op jit(solution)/shard_map/ppermute | solution.py:757
  8.2 5.1 %collective-permute-start = (f32[40,128]{1,0:T(8,128)S(1)}, f32[40,128]{1,0:T(8,128)S(1)}, u32[]{:S(2)}, u32[]{:S(2)}) collective-permute-start(f32[40,128]{1,0:T(8,128)S(1)} %get-tuple-element.24), channel_id=1, source_target_pairs={{4,0},{8,4},{12,8},{0,12},{5,1},{9,5},{13,9},{1,13},{6,2},{10,6},{... | collective-permute-start | bytes 61448 | tf_op jit(solution)/shard_map/ppermute | solution.py:750
  11.8 5.6 %collective-permute-start.1 = (f32[40,128]{1,0:T(8,128)S(1)}, f32[40,128]{1,0:T(8,128)S(1)}, u32[]{:S(2)}, u32[]{:S(2)}) collective-permute-start(f32[40,128]{1,0:T(8,128)S(1)} %get-tuple-element.25), channel_id=1, source_target_pairs={{0,4},{4,8},{8,12},{12,0},{1,5},{5,9},{9,13},{13,1},{2,6},{6,10},{... | collective-permute-start | bytes 61448 | tf_op jit(solution)/shard_map/ppermute | solution.py:751
  17.6 1.7 %collective-permute-start.2 = (f32[80,128]{1,0:T(8,128)S(1)}, f32[80,128]{1,0:T(8,128)S(1)}, u32[]{:S(2)}, u32[]{:S(2)}) collective-permute-start(f32[80,128]{1,0:T(8,128)S(1)} %get-tuple-element.27), channel_id=1, source_target_pairs={{1,0},{2,1},{3,2},{0,3},{5,4},{6,5},{7,6},{4,7},{9,8},{10,9},{11,1... | collective-permute-start | bytes 122888 | tf_op jit(solution)/shard_map/ppermute | solution.py:750
  17.7 3.9 %collective-permute-start.3 = (f32[80,128]{1,0:T(8,128)S(1)}, f32[80,128]{1,0:T(8,128)S(1)}, u32[]{:S(2)}, u32[]{:S(2)}) collective-permute-start(f32[80,128]{1,0:T(8,128)S(1)} %get-tuple-element.28), channel_id=1, source_target_pairs={{0,1},{1,2},{2,3},{3,0},{4,5},{5,6},{6,7},{7,4},{8,9},{9,10},{10,1... | collective-permute-start | bytes 122888 | tf_op jit(solution)/shard_map/ppermute | solution.py:751
  18.8 3.6 %copy-start = (f32[3,4096]{1,0:T(4,128)S(1)}, f32[3,4096]{1,0:T(4,128)}, u32[]{:S(2)}) copy-start(f32[3,4096]{1,0:T(4,128)} %refs_0_.4) | copy-start | bytes 147460
  18.8 3.5 %copy-start.1 = (s32[3,4096]{1,0:T(4,128)S(1)}, s32[3,4096]{1,0:T(4,128)}, u32[]{:S(2)}) copy-start(s32[3,4096]{1,0:T(4,128)} %refs_1_.3) | copy-start | bytes 147460
  18.8 6.8 %copy-start.2 = (s32[32]{0:T(128)S(1)}, s32[32]{0:T(128)}, u32[]{:S(2)}) copy-start(s32[32]{0:T(128)} %refs_0_.5) | copy-start | bytes 388
  21.8 3.9 %collective-permute-start.4 = (f32[48,128]{1,0:T(8,128)S(1)}, f32[48,128]{1,0:T(8,128)S(1)}, u32[]{:S(2)}, u32[]{:S(2)}) collective-permute-start(f32[48,128]{1,0:T(8,128)S(1)} %get-tuple-element.30), channel_id=1, source_target_pairs={{0,16},{16,0},{1,17},{17,1},{2,18},{18,2},{3,19},{19,3},{4,20},{20... | collective-permute-start | bytes 73736 | tf_op jit(solution)/shard_map/ppermute | solution.py:757

commit v3 on v2

--- a/solution.py
+++ b/solution.py
@@ -244,7 +244,6 @@
     grid_ref,
     low_ref,
     high_ref,
-    early_ref,
     tile_ref,
     count_ref,
     frac_ref,
@@ -376,26 +375,10 @@
 
     lax.fori_loop(0, blocks, one_block, 0, unroll=min(blocks, 32))
 
-    low = [jnp.zeros((8, BLOCK), jnp.float32) for _ in range(SPAN)]
-    high = [jnp.zeros((8, BLOCK), jnp.float32) for _ in range(SPAN)]
-    for group in range(GROUPS):
-        low_mask = lane // 2 == group
-        high_mask = lane // 2 == (CY // 2 + group) % 64
-        for spot in range(SPAN):
-            tile = group * SPAN + spot
-            if tile < TILES:
-                turned = roll(grid_ref[tile_rows(tile), :], 2 * group)
-                low[spot] = jnp.where(low_mask, turned, low[spot])
-                high[spot] = jnp.where(high_mask, turned, high[spot])
-    for spot in range(SPAN):
-        low_ref[tile_rows(spot), :] = low[spot]
-        high_ref[tile_rows(spot), :] = high[spot]
-    for side, start in enumerate((0, CX)):
-        planes = [
-            [grid_ref[tile_rows((start + part) * FACE + spot), :] for spot in range(FACE)]
-            for part in range(2)
-        ]
-        pack_pairs(planes[0], planes[1], early_ref, side * (FACE + 1))
+    half = PX // 2
+    for target, side in ((low_ref, 0), (high_ref, FACE - 1)):
+        faces = [grid_ref[tile_rows(step * FACE + side), :] for step in range(PX)]
+        pack_pairs(faces[:half], faces[half:], target)
     stress_copy.wait()
 
 
@@ -415,30 +398,66 @@
 RIM_TILES = [(part, spot) for part in range(2) for spot in range(1, FACE - 1)]
 
 
-def join_y_faces(above_ref, below_ref, _, grid_ref, low_ref, high_ref):
-    above = [above_ref[tile_rows(spot), :] for spot in range(SPAN)]
-    below = [below_ref[tile_rows(spot), :] for spot in range(SPAN)]
-    tiles = [step * FACE + side for step in range(PX) for side in (0, FACE - 1)]
-    add_y(grid_ref, above, below, tiles)
-    half = PX // 2
-    for target, side in ((low_ref, 0), (high_ref, FACE - 1)):
-        faces = [grid_ref[tile_rows(step * FACE + side), :] for step in range(PX)]
-        pack_pairs(faces[:half], faces[half:], target)
-
-
-def join_y_rest(above_ref, below_ref, _, grid_ref):
-    above = [above_ref[tile_rows(spot), :] for spot in range(SPAN)]
-    below = [below_ref[tile_rows(spot), :] for spot in range(SPAN)]
-    tiles = [step * FACE + side for step in range(PX) for side in range(1, FACE - 1)]
-    add_y(grid_ref, above, below, tiles)
-
-
-def join_z(above_ref, below_ref, _, grid_ref, late_ref):
+def pack_y(grid_ref, low, high, tiles):
+    lane = lane_index()
+    for group in range(GROUPS):
+        low_mask = lane // 2 == group
+        high_mask = lane // 2 == (CY // 2 + group) % 64
+        for spot in range(SPAN):
+            tile = group * SPAN + spot
+            if tile in tiles:
+                turned = roll(grid_ref[tile_rows(tile), :], 2 * group)
+                low[spot] = jnp.where(low_mask, turned, low[spot])
+                high[spot] = jnp.where(high_mask, turned, high[spot])
+
+
+Z_FACES = {step * FACE + side for step in range(PX) for side in (0, FACE - 1)}
+X_EDGES = {step * FACE + spot for step in (0, 1, CX, CX + 1) for spot in range(FACE)}
+
+
+def pack_kernel(grid_ref, low_ref, high_ref, early_ref):
+    for side, start in enumerate((0, CX)):
+        planes = [
+            [grid_ref[tile_rows((start + part) * FACE + spot), :] for spot in range(FACE)]
+            for part in range(2)
+        ]
+        pack_pairs(planes[0], planes[1], early_ref, side * (FACE + 1))
+    low = [jnp.zeros((8, BLOCK), jnp.float32) for _ in range(SPAN)]
+    high = [jnp.zeros((8, BLOCK), jnp.float32) for _ in range(SPAN)]
+    pack_y(grid_ref, low, high, set(range(TILES)) - Z_FACES)
+    for spot in range(SPAN):
+        low_ref[tile_rows(spot), :] = low[spot]
+        high_ref[tile_rows(spot), :] = high[spot]
+
+
+def join_z(above_ref, below_ref, part_low_ref, part_high_ref, _, grid_ref, low_ref, high_ref):
     half = PX // 2
     for source, side in ((below_ref, 0), (above_ref, FACE - 1)):
         first, second = unpack_pairs(source, half)
         for step, value in enumerate(first + second):
             grid_ref[tile_rows(step * FACE + side), :] += value
+    low = [part_low_ref[tile_rows(spot), :] for spot in range(SPAN)]
+    high = [part_high_ref[tile_rows(spot), :] for spot in range(SPAN)]
+    pack_y(grid_ref, low, high, Z_FACES)
+    for spot in range(SPAN):
+        low_ref[tile_rows(spot), :] = low[spot]
+        high_ref[tile_rows(spot), :] = high[spot]
+
+
+def read_tiles(source):
+    return [source[tile_rows(spot), :] for spot in range(SPAN)]
+
+
+def join_y_rest(above_ref, below_ref, _, grid_ref):
+    tiles = sorted(set(range(TILES)) - X_EDGES)
+    add_y(grid_ref, read_tiles(above_ref), read_tiles(below_ref), tiles)
+
+
+RIM_TILES = [(part, spot) for part in range(2) for spot in range(1, FACE - 1)]
+
+
+def join_y_edges(above_ref, below_ref, _, grid_ref, late_ref):
+    add_y(grid_ref, read_tiles(above_ref), read_tiles(below_ref), sorted(X_EDGES))
     lane = lane_index()
     for place, start in enumerate((0, CX)):
 
@@ -736,7 +755,7 @@
             copy.start()
         return carry
 
-    lax.fori_loop(0, chunk_count, one_chunk, 0)
+    lax.fori_loop(0, chunk_count, one_chunk, 0, unroll=min(chunk_count, 4))
     for chunk in range(chunk_count):
         copies += chunk_copies(chunk)
     for copy in copies:
@@ -797,17 +816,16 @@
         point_stress,
         mass,
     )
-    new_stress, grid, low, high, early = pl.pallas_call(
+    new_stress, grid, low, high = pl.pallas_call(
         lambda *refs: deposit_kernel(blocks, *refs),
         out_shape=(
             jax.ShapeDtypeStruct((6, points), f32),
             grid_shape,
-            message(SPAN),
-            message(SPAN),
-            message(2 * (FACE + 1)),
+            message(PX // 2 + 1),
+            message(PX // 2 + 1),
         ),
         in_specs=[hbm] * 8,
-        out_specs=(hbm,) + (vmem,) * 4,
+        out_specs=(hbm,) + (vmem,) * 3,
         scratch_shapes=[
             pltpu.SMEM(block_tile.shape, jnp.int32),
             pltpu.SMEM(block_count.shape, jnp.int32),
@@ -836,19 +854,54 @@
         name="weights",
     )
     weights = weigh(point_frac, cell_offset)
-    above, below = exchange(low, high, "gy")
+    above, below = exchange(low, high, "gz")
+    pack = pl.pallas_call(
+        pack_kernel,
+        out_shape=(message(SPAN), message(SPAN), message(2 * (FACE + 1))),
+        in_specs=[vmem],
+        out_specs=(vmem,) * 3,
+        compiler_params=params,
+        cost_estimate=cost(0.5),
+        name="pack_y",
+    )
+    low, high, early = pack(grid)
     early = exchange_both(early, "gx")
     grid, low, high = pl.pallas_call(
-        join_y_faces,
-        out_shape=(grid_shape, message(PX // 2 + 1), message(PX // 2 + 1)),
+        join_z,
+        out_shape=(grid_shape, message(SPAN), message(SPAN)),
+        in_specs=[vmem] * 5,
+        out_specs=(vmem,) * 3,
+        input_output_aliases={4: 0},
+        compiler_params=params,
+        cost_estimate=cost(0.3),
+        name="join_z",
+    )(above, below, low, high, grid)
+    above, below = exchange(low, high, "gy")
+    weigh = pl.pallas_call(
+        lambda *refs: weights_kernel(blocks, *refs),
+        out_shape=(
+            message(2 * blocks),
+            message(6 * blocks),
+            jax.ShapeDtypeStruct((32 * blocks, 2 * BLOCK), jnp.bfloat16),
+        ),
+        in_specs=[vmem] * 2,
+        out_specs=(vmem,) * 3,
+        compiler_params=params,
+        cost_estimate=cost(1),
+        name="weights",
+    )
+    weights = weigh(point_frac, cell_offset)
+    grid, late = pl.pallas_call(
+        join_y_edges,
+        out_shape=(grid_shape, message(6)),
         in_specs=[vmem] * 3,
-        out_specs=(vmem,) * 3,
+        out_specs=(vmem,) * 2,
         input_output_aliases={2: 0},
         compiler_params=params,
         cost_estimate=cost(0.3),
-        name="join_y_faces",
+        name="join_y_edges",
     )(above, below, grid)
-    grid = pl.pallas_call(
+    rest = pl.pallas_call(
         join_y_rest,
         out_shape=grid_shape,
         in_specs=[vmem] * 3,
@@ -857,18 +910,8 @@
         compiler_params=params,
         cost_estimate=cost(1),
         name="join_y_rest",
-    )(above, below, grid)
-    above, below = exchange(low, high, "gz")
-    grid, late = pl.pallas_call(
-        join_z,
-        out_shape=(grid_shape, message(6)),
-        in_specs=[vmem] * 3,
-        out_specs=(vmem,) * 2,
-        input_output_aliases={2: 0},
-        compiler_params=params,
-        cost_estimate=cost(0.3),
-        name="join_z",
-    )(above, below, grid)
+    )
+    grid = rest(above, below, grid)
     late = exchange_both(late, "gx")
     spread_shape = message(SPREADS * TILES)
     spread, inner, matrix, edge = pl.pallas_call(

time: 28.7 us -> 28.6 us (level)
  Pallas kernels: 10.3 us -> 10 us
    ppermute x2, waiting for transfers between devices: 1.98 us -> 3.16 us  [exchange(): above = lax.ppermute(low, axis, down)]
    ppermute x2, starting transfers between devices: 3.67 us -> 4.33 us  [exchange(): above = lax.ppermute(low, axis, down)]
    ppermute x2, waiting for transfers between devices: 1.31 us -> 0.72 us  [exchange_both(): return lax.ppermute(message, axis, [(0, 1), (1, 0)])]
    ppermute x2, waiting for transfers between devices: 6.34 us -> 5.84 us  [exchange(): below = lax.ppermute(high, axis, up)]
    ppermute x2, starting transfers between devices: 0.5 us -> 0.01 us  [exchange(): below = lax.ppermute(high, axis, up)]
    pallas_call x1, Pallas kernels: 4.51 us -> 4.06 us  [step(): pl.pallas_call(lambda *refs: deposit_kernel(blocks, *refs), out_shape=(ja...]
    pallas_call x3 -> x4, Pallas kernels: 1.01 us -> 1.44 us  [the longest x1 0.56 us: step(): grid = rest(above, below, grid)]
where the time goes in v3:
time: 28.6 us; the launch traced here: 28.4 us
  Pallas kernels  10 us (35%)
  waiting for transfers between devices  9.72 us (34%)
  starting transfers between devices  7.97 us (28%)
  between operations  0.7 us (2%)
    ppermute x2, waiting for transfers between devices, exchange(): below = lax.ppermute(high, axis, up)  5.84 us
    ppermute x2, starting transfers between devices, exchange(): above = lax.ppermute(low, axis, down)  4.33 us
    pallas_call x1, Pallas kernels, step(): pl.pallas_call(lambda *refs: deposit_kernel(blocks, *refs), out_shape=(ja...  4.06 us
    ppermute x2, starting transfers between devices, exchange_both(): return lax.ppermute(message, axis, [(0, 1), (1, 0)])  3.63 us
    ppermute x2, waiting for transfers between devices, exchange(): above = lax.ppermute(low, axis, down)  3.16 us
    pallas_call x1, Pallas kernels, step(): pl.pallas_call(lambda *refs: collect_kernel(blocks, *refs), out_shape=(sp...  2.58 us
    pallas_call x1, Pallas kernels, step(): pl.pallas_call(settle_kernel, out_shape=(spread_shape, out_shape, jax.Sha...  1.39 us
    ppermute x2, waiting for transfers between devices, exchange_both(): return lax.ppermute(message, axis, [(0, 1), (1, 0)])  0.72 us
  transfers between devices with their start and end apart: 6, of which 5 were waited for; matrix products, arithmetic and copies ran while one was open for 0% of the time, Pallas kernels for 10%

profile of v3, /device:TPU:0, one launch (start us, length us, event | category | flops | bytes accessed | tf_op | source)
XLA Modules:
  0.0 28.4 jit_solution(15060374645990429099)
XLA Ops:
  0.6 4.1 %deposit.1 = (f32[6,4096]{1,0:T(8,128)}, f32[2480,128]{1,0:T(8,128)S(1)}, f32[80,128]{1,0:T(8,128)S(1)}, f32[80,128]{1,0:T(8,128)S(1)}) custom-call(s32[32]{0:T(128)} %refs_0_.5, s32[32]{0:T(128)} %refs_1_.2, f32[3,4096]{1,0:T(4,128)} %refs_0_.4, s32[3,4096]{1,0:T(4,128)} %refs_1_.3, f32[3,4096]{1,0:T(4,128)} %refs_4_.1, f32[9,4096]{1,0:T(8,128)} %refs_5_.1, ...), custom_call_target="tpu_custom_call" | custom-call | flops 40000000 | bytes 1000 | tf_op jit(solution)/shard_map/deposit/pallas_call | solution.py:819
  4.7 0.4 %pack_y.1 = (f32[40,128]{1,0:T(8,128)S(1)}, f32[40,128]{1,0:T(8,128)S(1)}, f32[288,128]{1,0:T(8,128)S(1)}) custom-call(f32[2480,128]{1,0:T(8,128)S(1)} %get-tuple-element.28.grid_ref._), custom_call_target="tpu_custom_call" | custom-call | flops 4000000 | bytes 1000 | tf_op jit(solution)/shard_map/pack_y/pallas_call | solution.py:867
  5.1 3.0 %collective-permute-start.5 = (f32[288,128]{1,0:T(8,128)S(1)}, f32[288,128]{1,0:T(8,128)S(1)}, u32[]{:S(2)}, u32[]{:S(2)}) collective-permute-start(f32[288,128]{1,0:T(8,128)S(1)} %get-tuple-element.38), channel_id=1, source_target_pairs={{0,16},{16,0},{1,17},{17,1},{2,18},{18,2},{3,19},{19,3},{4,20},{20... | collective-permute-start | bytes 442376 | tf_op jit(solution)/shard_map/ppermute | solution.py:776
  8.2 0.7 %collective-permute-start = (f32[80,128]{1,0:T(8,128)S(1)}, f32[80,128]{1,0:T(8,128)S(1)}, u32[]{:S(2)}, u32[]{:S(2)}) collective-permute-start(f32[80,128]{1,0:T(8,128)S(1)} %get-tuple-element.26), channel_id=1, source_target_pairs={{1,0},{2,1},{3,2},{0,3},{5,4},{6,5},{7,6},{4,7},{9,8},{10,9},{11,1... | collective-permute-start | bytes 122888 | tf_op jit(solution)/shard_map/ppermute | solution.py:769
  8.8 0.0 collective-permute-start.1
  8.8 1.7 %collective-permute-done.above_ref = f32[80,128]{1,0:T(8,128)S(1)} collective-permute-done((f32[80,128]{1,0:T(8,128)S(1)}, f32[80,128]{1,0:T(8,128)S(1)}, u32[]{:S(2)}, u32[]{:S(2)}) %collective-permute-start) | collective-permute-done | bytes 40992 | tf_op jit(solution)/shard_map/ppermute | solution.py:769
  10.5 1.7 %collective-permute-done.1.below_ref = f32[80,128]{1,0:T(8,128)S(1)} collective-permute-done((f32[80,128]{1,0:T(8,128)S(1)}, f32[80,128]{1,0:T(8,128)S(1)}, u32[]{:S(2)}, u32[]{:S(2)}) %collective-permute-start.1) | collective-permute-done | bytes 40992 | tf_op jit(solution)/shard_map/ppermute | solution.py:770
  12.3 0.0 copy-start
  12.3 0.0 copy-start.1
  12.3 0.2 join_z.1
  12.4 3.7 %collective-permute-start.2 = (f32[40,128]{1,0:T(8,128)S(1)}, f32[40,128]{1,0:T(8,128)S(1)}, u32[]{:S(2)}, u32[]{:S(2)}) collective-permute-start(f32[40,128]{1,0:T(8,128)S(1)} %get-tuple-element.31), channel_id=1, source_target_pairs={{4,0},{8,4},{12,8},{0,12},{5,1},{9,5},{13,9},{1,13},{6,2},{10,6},{... | collective-permute-start | bytes 61448 | tf_op jit(solution)/shard_map/ppermute | solution.py:769
  16.1 0.0 collective-permute-start.3
  16.1 1.5 %collective-permute-done.2.above_ref = f32[40,128]{1,0:T(8,128)S(1)} collective-permute-done((f32[40,128]{1,0:T(8,128)S(1)}, f32[40,128]{1,0:T(8,128)S(1)}, u32[]{:S(2)}, u32[]{:S(2)}) %collective-permute-start.2) | collective-permute-done | bytes 20512 | tf_op jit(solution)/shard_map/ppermute | solution.py:769
  17.6 4.1 %collective-permute-done.3.below_ref = f32[40,128]{1,0:T(8,128)S(1)} collective-permute-done((f32[40,128]{1,0:T(8,128)S(1)}, f32[40,128]{1,0:T(8,128)S(1)}, u32[]{:S(2)}, u32[]{:S(2)}) %collective-permute-start.3) | collective-permute-done | bytes 20512 | tf_op jit(solution)/shard_map/ppermute | solution.py:770
  21.7 0.3 join_y_edges.1
  22.0 0.6 %collective-permute-start.4 = (f32[48,128]{1,0:T(8,128)S(1)}, f32[48,128]{1,0:T(8,128)S(1)}, u32[]{:S(2)}, u32[]{:S(2)}) collective-permute-start(f32[48,128]{1,0:T(8,128)S(1)} %get-tuple-element.34), channel_id=1, source_target_pairs={{0,16},{16,0},{1,17},{17,1},{2,18},{18,2},{3,19},{19,3},{4,20},{20... | collective-permute-start | bytes 73736 | tf_op jit(solution)/shard_map/ppermute | solution.py:776
  22.6 0.0 copy-done
  22.6 0.0 copy-done.1
  22.6 0.6 %weights.1 = (f32[512,128]{1,0:T(8,128)S(1)}, f32[1536,128]{1,0:T(8,128)S(1)}, bf16[1024,256]{1,0:T(8,128)(2,1)S(1)}) custom-call(f32[3,4096]{1,0:T(4,128)S(1)} %copy-done, s32[3,4096]{1,0:T(4,128)S(1)} %copy-done.1), custom_call_target="tpu_custom_call" | custom-call | flops 8000000 | bytes 1000 | tf_op jit(solution)/shard_map/weights/pallas_call | solution.py:893
  23.2 0.6 %join_y_rest.1.grid_ref = f32[2480,128]{1,0:T(8,128)S(1)} custom-call(f32[40,128]{1,0:T(8,128)S(1)} %collective-permute-done.2.above_ref, f32[40,128]{1,0:T(8,128)S(1)} %collective-permute-done.3.below_ref, f32[2480,128]{1,0:T(8,128)S(1)} %get-tuple-element.39._), custom_call_target="tpu_custom_call", output_to_operand_aliasing={{}: (2, {})} | custom-call | flops 8000000 | bytes 1000 | tf_op jit(solution)/shard_map/join_y_rest/pallas_call | solution.py:914
  23.7 0.0 copy-start.2
  23.7 0.0 collective-permute-done.5.source_ref
  23.7 1.4 %settle.1 = (f32[7344,128]{1,0:T(8,128)S(1)}, f32[3,16,32,64]{3,2,1,0:T(8,128)S(1)}, bf16[256,384]{1,0:T(8,128)(2,1)S(1)}, f32[544,128]{1,0:T(8,128)S(1)}) custom-call(f32[288,128]{1,0:T(8,128)S(1)} %collective-permute-done.5.source_ref, f32[2480,128]{1,0:T(8,128)S(1)} %join_y_rest.1.grid_ref), custom_call_target="tpu_custom_call" | custom-call | flops 16000000 | bytes 1000 | tf_op jit(solution)/shard_map/settle/pallas_call | solution.py:917
  25.1 0.7 %collective-permute-done.4.refs_1_ = f32[48,128]{1,0:T(8,128)S(1)} collective-permute-done((f32[48,128]{1,0:T(8,128)S(1)}, f32[48,128]{1,0:T(8,128)S(1)}, u32[]{:S(2)}, u32[]{:S(2)}) %collective-permute-start.4) | collective-permute-done | bytes 24608 | tf_op jit(solution)/shard_map/ppermute | solution.py:776
  25.9 0.0 copy-done.2
  25.9 2.6 %collect.1 = (f32[7344,128]{1,0:T(8,128)S(1)}, f32[3,16,32,64]{3,2,1,0:T(8,128)}, f32[3,4096]{1,0:T(4,128)}, f32[9,4096]{1,0:T(8,128)}) custom-call(s32[32]{0:T(128)S(1)} %copy-done.2, f32[48,128]{1,0:T(8,128)S(1)} %collective-permute-done.4.refs_1_, f32[512,128]{1,0:T(8,128)S(1)} %get-tuple-element.35.refs_2_, ...), custom_call_target="tpu_custom_call", output_to_operand_aliasing={{0}: (8, {})} | custom-call | flops 32000000 | bytes 1000 | tf_op jit(solution)/shard_map/collect/pallas_call | solution.py:932
Async XLA Ops:
  5.1 18.6 %collective-permute-start.5 = (f32[288,128]{1,0:T(8,128)S(1)}, f32[288,128]{1,0:T(8,128)S(1)}, u32[]{:S(2)}, u32[]{:S(2)}) collective-permute-start(f32[288,128]{1,0:T(8,128)S(1)} %get-tuple-element.38), channel_id=1, source_target_pairs={{0,16},{16,0},{1,17},{17,1},{2,18},{18,2},{3,19},{19,3},{4,20},{20... | collective-permute-start | bytes 442376 | tf_op jit(solution)/shard_map/ppermute | solution.py:776
  8.2 2.4 %collective-permute-start = (f32[80,128]{1,0:T(8,128)S(1)}, f32[80,128]{1,0:T(8,128)S(1)}, u32[]{:S(2)}, u32[]{:S(2)}) collective-permute-start(f32[80,128]{1,0:T(8,128)S(1)} %get-tuple-element.26), channel_id=1, source_target_pairs={{1,0},{2,1},{3,2},{0,3},{5,4},{6,5},{7,6},{4,7},{9,8},{10,9},{11,1... | collective-permute-start | bytes 122888 | tf_op jit(solution)/shard_map/ppermute | solution.py:769
  8.8 3.4 %collective-permute-start.1 = (f32[80,128]{1,0:T(8,128)S(1)}, f32[80,128]{1,0:T(8,128)S(1)}, u32[]{:S(2)}, u32[]{:S(2)}) collective-permute-start(f32[80,128]{1,0:T(8,128)S(1)} %get-tuple-element.27), channel_id=1, source_target_pairs={{0,1},{1,2},{2,3},{3,0},{4,5},{5,6},{6,7},{7,4},{8,9},{9,10},{10,1... | collective-permute-start | bytes 122888 | tf_op jit(solution)/shard_map/ppermute | solution.py:770
  12.3 10.3 %copy-start = (f32[3,4096]{1,0:T(4,128)S(1)}, f32[3,4096]{1,0:T(4,128)}, u32[]{:S(2)}) copy-start(f32[3,4096]{1,0:T(4,128)} %refs_0_.4) | copy-start | bytes 147460
  12.3 10.3 %copy-start.1 = (s32[3,4096]{1,0:T(4,128)S(1)}, s32[3,4096]{1,0:T(4,128)}, u32[]{:S(2)}) copy-start(s32[3,4096]{1,0:T(4,128)} %refs_1_.3) | copy-start | bytes 147460
  12.4 5.1 %collective-permute-start.2 = (f32[40,128]{1,0:T(8,128)S(1)}, f32[40,128]{1,0:T(8,128)S(1)}, u32[]{:S(2)}, u32[]{:S(2)}) collective-permute-start(f32[40,128]{1,0:T(8,128)S(1)} %get-tuple-element.31), channel_id=1, source_target_pairs={{4,0},{8,4},{12,8},{0,12},{5,1},{9,5},{13,9},{1,13},{6,2},{10,6},{... | collective-permute-start | bytes 61448 | tf_op jit(solution)/shard_map/ppermute | solution.py:769
  16.1 5.6 %collective-permute-start.3 = (f32[40,128]{1,0:T(8,128)S(1)}, f32[40,128]{1,0:T(8,128)S(1)}, u32[]{:S(2)}, u32[]{:S(2)}) collective-permute-start(f32[40,128]{1,0:T(8,128)S(1)} %get-tuple-element.32), channel_id=1, source_target_pairs={{0,4},{4,8},{8,12},{12,0},{1,5},{5,9},{9,13},{13,1},{2,6},{6,10},{... | collective-permute-start | bytes 61448 | tf_op jit(solution)/shard_map/ppermute | solution.py:770
  22.0 3.9 %collective-permute-start.4 = (f32[48,128]{1,0:T(8,128)S(1)}, f32[48,128]{1,0:T(8,128)S(1)}, u32[]{:S(2)}, u32[]{:S(2)}) collective-permute-start(f32[48,128]{1,0:T(8,128)S(1)} %get-tuple-element.34), channel_id=1, source_target_pairs={{0,16},{16,0},{1,17},{17,1},{2,18},{18,2},{3,19},{19,3},{4,20},{20... | collective-permute-start | bytes 73736 | tf_op jit(solution)/shard_map/ppermute | solution.py:776
  23.7 2.1 %copy-start.2 = (s32[32]{0:T(128)S(1)}, s32[32]{0:T(128)}, u32[]{:S(2)}) copy-start(s32[32]{0:T(128)} %refs_0_.5) | copy-start | bytes 388
